TPU v7x, 256 devices: a whole 4x4x8 slice. The times are simulated.
256 devices in a mesh: seq: 32 (over z, y), mp: 8 (over x, core).
Axes of the slice: x: 4, y: 4, z: 8, core: 2. Of those that a mesh axis runs over, the one named last changes fastest.
Arguments:
- ssm_input: bfloat16 [32768, 5120], P('seq', 'mp'), may hold values from -6 to 6
- gate_input: bfloat16 [32768, 5120], P('seq', 'mp'), may hold values from -6 to 6
- state_in: bfloat16 [32768, 128], P('seq'), may hold values from -6 to 6
- state_out: bfloat16 [32768, 128], P('seq'), may hold values from -0.5 to 0.5
- step_size: float32 [32768, 80], P('seq', 'mp'), may hold values from 0.05 to 0.2
- log_decay: float32 [32768, 80], P('seq', 'mp'), may hold values from -2 to 0
- skip_gain: float32 [80], P('mp'), may hold values from 0.5 to 2
- norm_gain: bfloat16 [5120], P('mp'), may hold values from 0.099609375 to 1.8984375
- out_weight: bfloat16 [5120, 2560], P('mp'), may hold values from -0.078125 to 0.078125
Outputs:
- layer_out: bfloat16 [32768, 2560], P(('seq', 'mp'))
All inputs are finite; a program needn't handle non-finite values.
Results may differ from a plain program's by a relative error of at most 0.011.
Values may be sent and summed in bfloat16 or wider, within the bound.
No kernel may reach another device: no remote copies, remote signals or barrier semaphores. Data moves between devices by JAX's collectives and lax.ppermute only.
A program may use at most 64 MiB of HBM per device.

v0:
```python
import functools

import jax
import jax.numpy as jnp
from jax import lax
from jax.experimental import pallas as pl
from jax.experimental.pallas import tpu as pltpu
from jax.sharding import Mesh
from jax.sharding import PartitionSpec as P


BLOCK = 256
HALF = 128
HEADS = 10
WIDTH = 64
CH = HEADS * WIDTH
STATE = 128
ROWS = 1024
NBLK = ROWS // BLOCK
SEQ_DEV = 32
PIECE = STATE // SEQ_DEV
D = 2560
DH = D // 2
PADH = 16
TALL = HALF + 8
LOG2E = 1.4426950408889634
F32 = jnp.float32
BF16 = jnp.bfloat16


def parts(value, count):
    out = []
    for _ in range(count):
        piece = value.astype(BF16)
        out.append(piece)
        value = value - piece.astype(F32)
    return out


def spread_matrix(count, tail):
    cols = CH + (HALF if tail else 0)
    row = lax.broadcasted_iota(jnp.int32, (PADH * count, cols), 0) % PADH
    col = lax.broadcasted_iota(jnp.int32, (PADH * count, cols), 1)
    head = jnp.where(col < CH, col // WIDTH, col - CH)
    return jnp.where(row == head, 1.0, 0.0).astype(BF16)


def spread(value, matrix, count):
    stacked = jnp.concatenate(parts(value, count), axis=0)
    return lax.dot_general(stacked, matrix, (((0,), (0,)), ((), ())), preferred_element_type=F32)


def triangle():
    row = lax.broadcasted_iota(jnp.int32, (BLOCK, BLOCK), 0)
    return jnp.where(row <= lax.broadcasted_iota(jnp.int32, (BLOCK, BLOCK), 1), 1.0, 0.0).astype(BF16)


def running_sums(value):
    rows = value.shape[0]
    sums = jnp.dot(jnp.concatenate(parts(value, 3), axis=0), triangle(), preferred_element_type=F32)
    return sums[0:rows] + sums[rows : 2 * rows] + sums[2 * rows : 3 * rows]


def state_kernel(
    x_hbm, b_hbm, dt_hbm, ld_hbm, msg_ref, pad_ref, dtp_ref, run_ref, x_ref, b_ref, dt_ref, ld_ref, sem
):
    copies = [pltpu.make_async_copy(ld_hbm, ld_ref, sem.at[0]), pltpu.make_async_copy(dt_hbm, dt_ref, sem.at[1])]
    for k in range(NBLK):
        rows = pl.ds(BLOCK * k, BLOCK)
        copies.append(pltpu.make_async_copy(x_hbm.at[rows, :], x_ref.at[rows, :], sem.at[2 + 2 * k]))
        copies.append(pltpu.make_async_copy(b_hbm.at[rows, :], b_ref.at[rows, :], sem.at[3 + 2 * k]))
    for copy in copies:
        copy.start()
    pad_ref[...] = jnp.zeros_like(pad_ref)
    dtp_ref[...] = jnp.zeros_like(dtp_ref)
    copies[0].wait()
    for k in range(NBLK):
        pad_ref[PADH * k : PADH * k + HEADS, :] = ld_ref[:, BLOCK * k : BLOCK * (k + 1)]
    levels = running_sums(pad_ref[...])
    closings = [levels[PADH * k : PADH * (k + 1), BLOCK - 1 : BLOCK] for k in range(NBLK)]
    tails = [jnp.zeros((PADH, 1), F32)]
    for k in reversed(range(NBLK)):
        tails.insert(0, tails[0] + closings[k])
    lane = lax.broadcasted_iota(jnp.int32, (PADH, HALF), 1)
    decay = spread(jnp.where(lane == 0, tails[0], 0.0), spread_matrix(3, True)[:, CH:], 3)[0:1, :]
    decays = jnp.concatenate([v.astype(F32) for v in parts(decay, 3)] + [jnp.zeros((1, HALF), F32)], axis=0)
    decays = decays.astype(BF16)
    two = spread_matrix(2, False)
    copies[1].wait()
    dtp_ref[0:HEADS, :] = dt_ref[...]
    total = None
    for k in range(NBLK):
        weight = jnp.exp(tails[k] - levels[PADH * k : PADH * (k + 1)]) * dtp_ref[:, BLOCK * k : BLOCK * (k + 1)]
        wide = spread(weight, two, 2)
        copies[2 + 2 * k].wait()
        copies[3 + 2 * k].wait()
        weighted = (wide * x_ref[BLOCK * k : BLOCK * (k + 1), :].astype(F32)).astype(BF16)
        own = lax.dot_general(
            b_ref[BLOCK * k : BLOCK * (k + 1), :], weighted, (((0,), (0,)), ((), ())), preferred_element_type=F32
        )
        total = own if total is None else total + own
    run_ref[...] = total
    for q in range(SEQ_DEV):
        msg_ref[q, :, 0:CH] = run_ref[PIECE * q : PIECE * (q + 1), :].astype(BF16)
        msg_ref[q, :, CH : CH + HALF] = decays


def prefix_kernel(msg_ref, out_ref, dec_ref):
    for i in range(SEQ_DEV):
        for part in range(3):
            dec_ref[part, i : i + 1, :] = msg_ref[i, :, CH : CH + HALF].astype(F32)[part : part + 1]
    head = lax.broadcasted_iota(jnp.int32, (HALF, CH), 0)
    col = lax.broadcasted_iota(jnp.int32, (HALF, CH), 1)
    matrix = jnp.where(head == col // WIDTH, 1.0, 0.0).astype(BF16)
    logs = jnp.zeros((SEQ_DEV, CH), F32)
    for part in range(3):
        logs = logs + jnp.dot(dec_ref[part].astype(BF16), matrix, preferred_element_type=F32)
    decay = jnp.exp(logs)
    running = jnp.zeros((PIECE, CH), F32)
    for i in range(SEQ_DEV):
        out_ref[i] = running.astype(BF16)
        running = decay[i : i + 1, :] * running + msg_ref[i, :, 0:CH].astype(F32)


def local_kernel(x_ref, g_ref, b_ref, c_ref, dt_ref, ld_ref, skip_ref, gl_ref, fs_ref, run_ref, lead_ref, pad_ref, dtp_ref):
    k = pl.program_id(0)

    @pl.when(k == 0)
    def _():
        run_ref[...] = jnp.zeros_like(run_ref)
        lead_ref[...] = jnp.zeros_like(lead_ref)
        pad_ref[...] = jnp.zeros_like(pad_ref)
        dtp_ref[...] = jnp.zeros_like(dtp_ref)

    pad_ref[0:HEADS, :] = ld_ref[...]
    dtp_ref[0:HEADS, :] = dt_ref[...]
    lev = running_sums(pad_ref[...])
    closing = lev[:, BLOCK - 1 : BLOCK]
    reader, writer = c_ref[...], b_ref[...]
    two = spread_matrix(2, False)
    lane = lax.broadcasted_iota(jnp.int32, (PADH, HALF), 1)
    table = jnp.where(lane == 0, jnp.exp(lead_ref[...]), jnp.where(lane == 1, jnp.exp(closing), 0.0))
    table = spread(table, spread_matrix(3, False), 3)
    lead = table[0:1, :]
    lead_ref[...] += closing
    grown = spread(jnp.exp(lev), two, 2)
    carry = jnp.dot(reader, run_ref[...].astype(BF16), preferred_element_type=F32)
    weight = spread(jnp.exp(closing - lev) * dtp_ref[...], two, 2)
    weighted = (weight * x_ref[...].astype(F32)).astype(BF16)
    own = lax.dot_general(writer, weighted, (((0,), (0,)), ((), ())), preferred_element_type=F32)
    run_ref[...] = table[1:2, :] * run_ref[...] + own
    lev2 = lev * LOG2E
    cols = jnp.transpose(lev2)
    rows = lev2[0:HEADS] - jnp.log(dt_ref[...]) * LOG2E
    inter = lax.dot_general(reader, writer, (((1,), (1,)), ((), ())), preferred_element_type=F32)
    causal = lax.broadcasted_iota(jnp.int32, (HALF, HALF), 0) >= lax.broadcasted_iota(jnp.int32, (HALF, HALF), 1)
    lane = lax.broadcasted_iota(jnp.int32, (HALF, HALF), 1) < WIDTH

    def score(head, r, s):
        gap = cols[HALF * r : HALF * (r + 1), head : head + 1] - rows[head : head + 1, HALF * s : HALF * (s + 1)]
        value = jnp.exp2(gap) * inter[HALF * r : HALF * (r + 1), HALF * s : HALF * (s + 1)]
        if r == s:
            value = jnp.where(causal, value, 0.0)
        return value.astype(BF16)

    for pair in range(HEADS // 2):
        lanes = slice(HALF * pair, HALF * (pair + 1))
        top_x = x_ref[0:HALF, lanes]
        low_x = x_ref[HALF:BLOCK, lanes]
        tops, lows = [], []
        for head in (2 * pair, 2 * pair + 1):
            tops.append(jnp.dot(score(head, 0, 0), top_x, preferred_element_type=F32))
            lows.append(
                jnp.dot(score(head, 1, 0), top_x, preferred_element_type=F32)
                + jnp.dot(score(head, 1, 1), low_x, preferred_element_type=F32)
            )
        for r, (even, odd), x_part in ((0, tops, top_x), (1, lows, low_x)):
            span = slice(HALF * r, HALF * (r + 1))
            mixed = (
                jnp.where(lane, even, odd)
                + grown[span, lanes] * carry[span, lanes]
                + skip_ref[:, lanes] * x_part.astype(F32)
            )
            gate = g_ref[span, lanes].astype(F32)
            gate = gate / (1.0 + jnp.exp(-gate))
            out_rows = pl.ds(pl.multiple_of(k * BLOCK + HALF * r, HALF), HALF)
            gl_ref[out_rows, lanes] = (mixed * gate).astype(BF16)
            fs_ref[out_rows, lanes] = (grown[span, lanes] * lead[:, lanes] * gate).astype(BF16)


def square_rows(total):
    rows = [piece.astype(F32) for piece in parts(total, 3)]
    return jnp.concatenate(rows + [jnp.zeros((8 - len(rows), HALF), F32)], axis=0).astype(BF16)


def squares_of(ref, first):
    return jnp.sum(ref[first : first + 8, 0:HALF].astype(F32), axis=0, keepdims=True)


def gate_kernel(first, count, idx_ref, p_ref, gain_ref, c_ref, gl_ref, fs_ref, *rest):
    fetch = None
    if len(rest) > 2:
        w_hbm, rows_ref, square_ref, p_out_ref, w_ref, st_ref, sem = rest
        fetch = pltpu.make_async_copy(w_hbm.at[:, 0:DH], w_ref, sem.at[0])
        fetch.start()
        for q in range(SEQ_DEV):
            st_ref[PIECE * q : PIECE * (q + 1), :] = p_ref[q].astype(F32)
        state = st_ref[...].astype(BF16)
        p_out_ref[...] = state
    else:
        rows_ref, square_ref = rest
        state = p_ref[...]
    gain = gain_ref[...]
    squares = []
    for side, half in enumerate((1 - idx_ref[0], idx_ref[0])):
        for i in range(count):
            rows = pl.ds(pl.multiple_of((2 * idx_ref[first + i] + half) * HALF, HALF), HALF)
            gated = gl_ref[rows, :].astype(F32) + fs_ref[rows, :].astype(F32) * jnp.dot(
                c_ref[rows, :], state, preferred_element_type=F32
            )
            sums = jnp.sum(gated * gated, axis=1, keepdims=True)
            squares.append(jnp.transpose(jnp.broadcast_to(sums, (HALF, HALF)))[0:1, :])
            place = count * side + i
            rows_ref[HALF * place : HALF * (place + 1), :] = (gated * gain).astype(BF16)
    square_ref[...] = jnp.concatenate(squares + [jnp.zeros((8 - len(squares), HALF), F32)], axis=0)
    if fetch is not None:
        fetch.wait()


def put_squares(ref, base, total):
    ref[base : base + TALL - HALF, 0:HALF] = square_rows(total)
    ref[base : base + TALL - HALF, HALF:DH] = jnp.zeros((TALL - HALF, DH - HALF), BF16)


def product_kernel(rows_ref, square_ref, w_ref, *rest):
    fetch = None
    if len(rest) > 2:
        w_hbm, send_ref, keep_ref, w_next_ref, sem = rest
        fetch = pltpu.make_async_copy(w_hbm.at[:, DH:D], w_next_ref, sem.at[0])
        fetch.start()
    else:
        send_ref, keep_ref = rest
    count = rows_ref.shape[0] // (2 * HALF)
    tall = send_ref.shape[0] // count
    rows = rows_ref[...]
    for j in range(DH // BLOCK):
        cols = slice(BLOCK * j, BLOCK * (j + 1))
        value = jnp.dot(rows, w_ref[:, cols], preferred_element_type=F32)
        keep_ref[:, cols] = value[HALF * count : 2 * HALF * count]
        for i in range(count):
            send_ref[tall * i : tall * i + HALF, cols] = value[HALF * i : HALF * (i + 1)].astype(BF16)
    if tall == TALL:
        for i in range(count):
            put_squares(send_ref, tall * i + HALF, square_ref[i : i + 1, :])
    if fetch is not None:
        fetch.wait()


def join_kernel(place, keep_ref, got_ref, *refs):
    out_ref = refs[-1]
    count = keep_ref.shape[0] // HALF
    tall = got_ref.shape[0] // count
    value = keep_ref[HALF * place : HALF * (place + 1), :] + got_ref[tall * place : tall * place + HALF, :].astype(F32)
    squares = tall == TALL
    more = refs[squares:-1]
    for ref in more:
        value = value + ref[0:HALF, :].astype(F32)
    out_ref[0:HALF, :] = value.astype(BF16)
    if squares:
        total = refs[0][count + place : count + place + 1, :] + squares_of(got_ref, tall * place + HALF)
        for ref in more:
            total = total + squares_of(ref, HALF)
        put_squares(out_ref, HALF, total)


def finish_kernel(devices, square_ref, ka_ref, kb_ref, ga_ref, gb_ref, ra_ref, la_ref, rb_ref, lb_ref, out_ref, scale_ref):
    rows = out_ref.shape[0]
    count = ka_ref.shape[0] // HALF
    last = count - 1

    @pl.when(pl.program_id(0) == 0)
    def _():
        total = square_ref[count + last : count + last + 1, :] + squares_of(ga_ref, TALL * last + HALF)
        total = total + squares_of(ra_ref, HALF) + squares_of(la_ref, HALF)
        scale = lax.rsqrt(total / (CH * devices) + 1e-05)
        scale_ref[...] = jnp.transpose(jnp.broadcast_to(scale, (HALF, HALF)))

    def part(ref, tall):
        return ref[pl.ds(pl.multiple_of(pl.program_id(0) * rows + tall * last, 8), rows), :].astype(F32)

    span = pl.ds(pl.multiple_of(pl.program_id(0) * rows, rows), rows)
    scale = scale_ref[span, 0:1]
    for i, (keep, got, tall, one, two) in enumerate(
        ((ka_ref, ga_ref, TALL, ra_ref, la_ref), (kb_ref, gb_ref, HALF, rb_ref, lb_ref))
    ):
        value = part(keep, HALF) + part(got, tall) + one[span, :].astype(F32) + two[span, :].astype(F32)
        out_ref[:, DH * i : DH * (i + 1)] = (value * scale).astype(BF16)


VMEM = pl.BlockSpec(memory_space=pltpu.VMEM)
SMEM = pl.BlockSpec(memory_space=pltpu.SMEM)
HBM = pl.BlockSpec(memory_space=pltpu.HBM)
LIMIT = 24 * 1024 * 1024


def local_call(kernel, args, outs, scratch=(), flops=1e8, in_specs=None, out_specs=None):
    in_specs, out_specs = in_specs or [VMEM] * len(args), out_specs or [VMEM] * len(outs)
    args = [pltpu.with_memory_space_constraint(v, pltpu.HBM) if spec is HBM else v for v, spec in zip(args, in_specs)]
    return pl.pallas_call(
        kernel,
        in_specs=in_specs,
        out_specs=out_specs,
        out_shape=[
            pltpu.HBM(*out) if spec is HBM else jax.ShapeDtypeStruct(*out) for out, spec in zip(outs, out_specs)
        ],
        scratch_shapes=[pltpu.VMEM(*v) if isinstance(v, tuple) else pltpu.SemaphoreType.DMA((v,)) for v in scratch],
        cost_estimate=pl.CostEstimate(flops=int(flops), bytes_accessed=0, transcendentals=0),
        compiler_params=pltpu.CompilerParams(vmem_limit_bytes=LIMIT),
    )(*args)


def local_state(x, b, dt, ld):
    outs = (((SEQ_DEV, PIECE, CH + HALF), BF16),)
    scratch = [
        ((PADH * NBLK, BLOCK), F32),
        ((PADH, ROWS), F32),
        ((STATE, CH), F32),
        ((ROWS, CH), BF16),
        ((ROWS, STATE), BF16),
        ((HEADS, ROWS), F32),
        ((HEADS, ROWS), F32),
        2 + 2 * NBLK,
    ]
    return local_call(state_kernel, (x, b, dt, ld), outs, scratch, 1e9, [HBM] * 4)[0]


def seq_prefix(msg):
    outs = (((SEQ_DEV, PIECE, CH), BF16),)
    scratch = [((3, SEQ_DEV, HALF), F32)]
    return local_call(prefix_kernel, (msg,), outs, scratch)[0]


def whole(shape):
    return pl.BlockSpec(shape, lambda *_: (0,) * len(shape))


def local_part(x, g, b, c, dt, ld, skip):
    rows = lambda width: pl.BlockSpec((BLOCK, width), lambda k: (k, 0))
    heads = pl.BlockSpec((HEADS, BLOCK), lambda k: (0, k))
    return pl.pallas_call(
        local_kernel,
        grid=(NBLK,),
        in_specs=[rows(CH), rows(CH), rows(STATE), rows(STATE), heads, heads, whole((1, CH))],
        out_specs=(VMEM, VMEM),
        out_shape=(jax.ShapeDtypeStruct((ROWS, CH), BF16), jax.ShapeDtypeStruct((ROWS, CH), BF16)),
        scratch_shapes=[
            pltpu.VMEM((STATE, CH), F32),
            pltpu.VMEM((PADH, HALF), F32),
            pltpu.VMEM((PADH, BLOCK), F32),
            pltpu.VMEM((PADH, BLOCK), F32),
        ],
        cost_estimate=pl.CostEstimate(flops=int(3e9), bytes_accessed=0, transcendentals=0),
        compiler_params=pltpu.CompilerParams(vmem_limit_bytes=LIMIT),
        name="local_part",
    )(*(pltpu.with_memory_space_constraint(v, pltpu.HBM) for v in (x, g, b, c, dt, ld)), skip)


def gated_rows(order, first, count, prefix, gain, c, gl, fs, *w):
    outs = [((2 * HALF * count, CH), BF16), ((8, HALF), F32)]
    scratch = []
    in_specs = [SMEM] + [VMEM] * 5 + [HBM] * len(w)
    if w:
        outs += [((STATE, CH), BF16), ((CH, DH), BF16)]
        scratch = [((STATE, CH), F32), 1]
    kernel = functools.partial(gate_kernel, first, count)
    return local_call(kernel, (order, prefix, gain, c, gl, fs, *w), outs, scratch, 5e8 * count, in_specs)


def product(rows, squares, w, tall, *w_next):
    count = rows.shape[0] // (2 * HALF)
    outs = [((tall * count, DH), BF16), ((HALF * count, DH), F32)] + [((CH, DH), BF16)] * len(w_next)
    in_specs = [VMEM] * 3 + [HBM] * len(w_next)
    flops = 2 * rows.shape[0] * CH * DH
    return local_call(product_kernel, (rows, squares, w, *w_next), outs, [1] * len(w_next), flops, in_specs)


def join(place, keep, got, *more):
    tall = got.shape[0] * HALF // keep.shape[0]
    return local_call(functools.partial(join_kernel, place), (keep, got, *more), (((tall, DH), BF16),))[0]


def finish(devices, *args):
    rows = 32
    return pl.pallas_call(
        functools.partial(finish_kernel, devices),
        grid=(HALF // rows,),
        in_specs=[VMEM] * len(args),
        out_specs=pl.BlockSpec((rows, D), lambda i: (i, 0)),
        out_shape=jax.ShapeDtypeStruct((HALF, D), BF16),
        scratch_shapes=[pltpu.VMEM((HALF, HALF), F32)],
        compiler_params=pltpu.CompilerParams(vmem_limit_bytes=LIMIT),
        name="finish",
    )(*args)


def after(value, earlier):
    return lax.optimization_barrier((value, earlier))[0]


def body(x, g, b, c, dt, ld, skip, gain, w):
    chips = lax.axis_size("x")
    chip, core = lax.axis_index("x"), lax.axis_index("c")
    up = [(i, (i + 1) % chips) for i in range(chips)]
    down = [(i, (i - 1) % chips) for i in range(chips)]
    swap = [(0, 1), (1, 0)]
    far, right, left = (chip + 2) % chips, (chip + 1) % chips, (chip + 3) % chips
    order = jnp.stack([core, far, right, left, chip]).astype(jnp.int32)
    msg = local_state(x, b, dt.T, ld.T)
    msg = lax.all_to_all(msg, ("z", "y"), split_axis=0, concat_axis=0, tiled=True)
    skip_wide = jnp.repeat(skip, WIDTH)[None, :]
    gl, fs = local_part(x, g, b, c, dt.T, ld.T, skip_wide)
    prefix = lax.all_to_all(seq_prefix(msg), ("z", "y"), split_axis=0, concat_axis=0, tiled=True)
    gain_row = gain.astype(F32)[None, :]

    rows0, square0, prefix, w_a = gated_rows(order, 1, 1, prefix, gain_row, c, gl, fs, w)
    send_a, keep_a, w_b = product(rows0, square0, w_a, TALL, w)
    got_a = lax.ppermute(send_a, "c", swap)
    send_b, keep_b = product(after(rows0, send_a), square0, w_b, HALF)
    got_b = lax.ppermute(send_b, "c", swap)
    rows1, square1 = gated_rows(order, 2, 3, after(prefix, send_b), gain_row, c, gl, fs)
    far_a = join(0, after(keep_a, rows1), got_a, square0)
    far_b = join(0, after(keep_b, far_a), got_b)
    rows1 = after(rows1, far_b)
    far_a, far_b = lax.ppermute(far_a, "x", up), lax.ppermute(far_b, "x", down)
    send_b, keep_b = product(rows1, square1, w_b, HALF)
    got_b = lax.ppermute(send_b, "c", swap)
    send_a, keep_a = product(after(rows1, send_b), square1, w_a, TALL)
    got_a = lax.ppermute(send_a, "c", swap)
    right_b = join(0, after(keep_b, send_a), got_b)
    left_a = join(1, after(keep_a, right_b), got_a, square1)
    right_a = join(0, after(keep_a, left_a), got_a, square1, far_a)
    left_b = join(1, after(keep_b, right_a), got_b, far_b)
    right_b, left_a = lax.ppermute(right_b, "x", up), lax.ppermute(left_a, "x", down)
    right_a, left_b = lax.ppermute(right_a, "x", up), lax.ppermute(left_b, "x", down)
    return finish(2 * chips, square1, keep_a, keep_b, got_a, got_b, right_a, left_a, right_b, left_b)


def solution(mesh):
    torus = Mesh(mesh.devices.reshape(8, 4, 4, 2), ("z", "y", "x", "c"))
    seq, mp = ("z", "y"), ("x", "c")
    in_specs = (
        P(seq, mp),
        P(seq, mp),
        P(seq, None),
        P(seq, None),
        P(seq, mp),
        P(seq, mp),
        P(mp),
        P(mp),
        P(mp, None),
    )

    return jax.shard_map(body, mesh=torus, in_specs=in_specs, out_specs=P(seq + mp, None), check_vma=False)
```

profile of v0, /device:TPU:6, one launch (start us, length us, event | category | flops | bytes accessed | tf_op | source)
XLA Modules:
  0.0 83.6 jit_solution(12415455151767593117)
XLA Ops:
  0.0 0.0 copy-start.1
  0.0 0.0 copy-start.2
  0.0 3.2 %shard_map.91 = bf16[32,4,768]{2,1,0:T(4,128)(2,1)S(1)} custom-call(bf16[1024,640]{1,0:T(8,128)(2,1)} %x_ref.1, bf16[1024,128]{1,0:T(8,128)(2,1)} %b_ref.1, f32[10,1024]{1,0:T(8,128)} %bitcast.7, f32[10,1024]{1,0:T(8,128)} %bitcast.9), custom_call_target="tpu_custom_call" | custom-call | flops 1000000000 | tf_op jit(solution)/shard_map/pallas_call | solution.py:309
  3.2 22.9 %all_to_all.10.msg_ref = bf16[32,4,768]{2,1,0:T(4,128)(2,1)S(1)} all-to-all(bf16[32,4,768]{2,1,0:T(4,128)(2,1)S(1)} %shard_map.91), channel_id=1, replica_groups=mesh['z'=8,'y'=4,'x'=4,'c'=2] {'z','y'}, dimensions={0} | all-to-all | bytes 393216 | tf_op jit(solution)/shard_map/all_to_all | solution.py:419
  26.1 1.0 %shard_map.92 = bf16[32,4,640]{2,1,0:T(4,128)(2,1)} custom-call(bf16[32,4,768]{2,1,0:T(4,128)(2,1)S(1)} %all_to_all.10.msg_ref), custom_call_target="tpu_custom_call" | custom-call | flops 100000000 | tf_op jit(solution)/shard_map/pallas_call | solution.py:309
  27.1 3.9 %all-to-all-start.1 = ((bf16[32,4,640]{2,1,0:T(4,128)(2,1)}), bf16[32,4,640]{2,1,0:T(4,128)(2,1)S(1)}, u32[]{:S(2)}, u32[]{:S(2)}) async-start(bf16[32,4,640]{2,1,0:T(4,128)(2,1)} %shard_map.92), calls=%async_computation.1 | async-start | bytes 327680 | tf_op jit(solution)/shard_map/all_to_all | solution.py:422
  31.0 0.0 copy-done.1
  31.0 0.0 copy-done.2
  31.0 0.1 broadcast_in_dim.10
  31.1 0.1 broadcast_in_dim_reshape.3.skip_ref
  31.2 0.1 stack.23.idx_ref
  31.3 0.0 copy-start
  31.3 7.5 %local_part.1 = (bf16[1024,640]{1,0:T(8,128)(2,1)S(1)}, bf16[1024,640]{1,0:T(8,128)(2,1)S(1)}) custom-call(bf16[1024,640]{1,0:T(8,128)(2,1)} %x_ref.1, bf16[1024,640]{1,0:T(8,128)(2,1)} %g_ref.1, bf16[1024,128]{1,0:T(8,128)(2,1)} %b_ref.1, bf16[1024,128]{1,0:T(8,128)(2,1)} %c_ref.5, f32[10,1024]{1,0:T(8,128)} %bitcast.8, f32[10,1024]{1,0:T(8,128)} %bitcast.10, ...), custom_call_target="tpu_custom_call" | custom-call | flops 3000000000 | tf_op jit(solution)/shard_map/local_part/pallas_call | solution.py:350
  38.7 3.2 %all-to-all-done.1.p_ref = bf16[32,4,640]{2,1,0:T(4,128)(2,1)S(1)} async-done(((bf16[32,4,640]{2,1,0:T(4,128)(2,1)}), bf16[32,4,640]{2,1,0:T(4,128)(2,1)S(1)}, u32[]{:S(2)}, u32[]{:S(2)}) %all-to-all-start.1) | async-done | bytes 163872 | tf_op jit(solution)/shard_map/all_to_all | solution.py:422
  41.9 0.0 copy-done
  41.9 2.1 %shard_map.93 = (bf16[256,640]{1,0:T(8,128)(2,1)S(1)}, f32[8,128]{1,0:T(8,128)S(1)}, bf16[128,640]{1,0:T(8,128)(2,1)S(1)}, bf16[640,1280]{1,0:T(8,128)(2,1)S(1)}) custom-call(s32[5]{0:T(128)S(1)} %stack.23.idx_ref, bf16[32,4,640]{2,1,0:T(4,128)(2,1)S(1)} %all-to-all-done.1.p_ref, f32[1,640]{1,0:T(1,128)S(1)} %reshape.gain_ref, ...), custom_call_target="tpu_custom_call" | custom-call | flops 500000000 | tf_op jit(solution)/shard_map/pallas_call | solution.py:309
  44.0 1.5 %shard_map.94 = (bf16[136,1280]{1,0:T(8,128)(2,1)S(1)}, f32[128,1280]{1,0:T(8,128)S(1)}, bf16[640,1280]{1,0:T(8,128)(2,1)S(1)}) custom-call(bf16[256,640]{1,0:T(8,128)(2,1)S(1)} %get-tuple-element.39.rows_ref, f32[8,128]{1,0:T(8,128)S(1)} %get-tuple-element.36.square_ref.refs_0_, bf16[640,1280]{1,0:T(8,128)(2,1)S(1)} %get-tuple-element.37.w_ref, ...), custom_call_target="tpu_custom_call" | custom-call | flops 419430400 | tf_op jit(solution)/shard_map/pallas_call | solution.py:309
  45.5 0.1 collective-permute-start
  45.6 0.7 shard_map.95
  46.3 0.6 collective-permute-start.1
  46.9 1.3 %shard_map.96 = (bf16[768,640]{1,0:T(8,128)(2,1)S(1)}, f32[8,128]{1,0:T(8,128)S(1)}) custom-call(s32[5]{0:T(128)S(1)} %stack.23.idx_ref, bf16[128,640]{1,0:T(8,128)(2,1)S(1)} %get-tuple-element.42.p_ref, f32[1,640]{1,0:T(1,128)S(1)} %reshape.gain_ref, bf16[1024,128]{1,0:T(8,128)(2,1)S(1)} %copy-done, bf16[1024,640]{1,0:T(8,128)(2,1)S(1)} %get-tuple-element.32.gl_ref, ...), custom_call_target="tpu_custom_call" | custom-call | flops 1500000000 | tf_op jit(solution)/shard_map/pallas_call | solution.py:309
  48.2 0.0 collective-permute-done.got_ref
  48.2 0.1 shard_map.97
  48.3 0.0 collective-permute-done.1.got_ref
  48.3 0.1 shard_map.98
  48.4 1.7 %shard_map.99 = (bf16[384,1280]{1,0:T(8,128)(2,1)S(1)}, f32[384,1280]{1,0:T(8,128)S(1)}) custom-call(bf16[768,640]{1,0:T(8,128)(2,1)S(1)} %get-tuple-element.51.rows_ref, f32[8,128]{1,0:T(8,128)S(1)} %get-tuple-element.43.square_ref.refs_0_, bf16[640,1280]{1,0:T(8,128)(2,1)S(1)} %get-tuple-element.40.w_ref), custom_call_target="tpu_custom_call" | custom-call | flops 1258291200 | tf_op jit(solution)/shard_map/pallas_call | solution.py:309
  50.1 1.7 %shard_map.100 = (bf16[408,1280]{1,0:T(8,128)(2,1)S(1)}, f32[384,1280]{1,0:T(8,128)S(1)}) custom-call(bf16[768,640]{1,0:T(8,128)(2,1)S(1)} %get-tuple-element.51.rows_ref, f32[8,128]{1,0:T(8,128)S(1)} %get-tuple-element.43.square_ref.refs_0_, bf16[640,1280]{1,0:T(8,128)(2,1)S(1)} %get-tuple-element.37.w_ref), custom_call_target="tpu_custom_call" | custom-call | flops 1258291200 | tf_op jit(solution)/shard_map/pallas_call | solution.py:309
  51.8 0.3 collective-permute-start.2
  52.0 0.3 collective-permute-start.3
  52.4 0.5 collective-permute-start.4
  52.9 1.5 %collective-permute-start.8 = (bf16[128,1280]{1,0:T(8,128)(2,1)S(1)}, bf16[128,1280]{1,0:T(8,128)(2,1)S(1)}, u32[]{:S(2)}, u32[]{:S(2)}) collective-permute-start(bf16[128,1280]{1,0:T(8,128)(2,1)S(1)} %shard_map.98), channel_id=1, source_target_pairs={{0,6},{2,0},{4,2},{6,4},{1,7},{3,1},{5,3},{7,5},{8,14},{10,8},{12,... | collective-permute-start | bytes 983048 | tf_op jit(solution)/shard_map/ppermute | solution.py:434
  54.4 1.5 %collective-permute-done.3.got_ref.gb_ref = bf16[384,1280]{1,0:T(8,128)(2,1)S(1)} collective-permute-done((bf16[384,1280]{1,0:T(8,128)(2,1)S(1)}, bf16[384,1280]{1,0:T(8,128)(2,1)S(1)}, u32[]{:S(2)}, u32[]{:S(2)}) %collective-permute-start.3) | collective-permute-done | bytes 983072 | tf_op jit(solution)/shard_map/ppermute | solution.py:436
  55.9 0.1 shard_map.101
  56.0 0.0 collective-permute-done.2.got_ref.ga_ref
  56.0 0.1 shard_map.102
  56.1 6.5 %collective-permute-done.4.refs_1_ = bf16[136,1280]{1,0:T(8,128)(2,1)S(1)} collective-permute-done((bf16[136,1280]{1,0:T(8,128)(2,1)S(1)}, bf16[136,1280]{1,0:T(8,128)(2,1)S(1)}, u32[]{:S(2)}, u32[]{:S(2)}) %collective-permute-start.4) | collective-permute-done | bytes 348192 | tf_op jit(solution)/shard_map/ppermute | solution.py:434
  62.6 0.1 shard_map.103
  62.7 1.8 %collective-permute-start.5 = (bf16[136,1280]{1,0:T(8,128)(2,1)S(1)}, bf16[136,1280]{1,0:T(8,128)(2,1)S(1)}, u32[]{:S(2)}, u32[]{:S(2)}) collective-permute-start(bf16[136,1280]{1,0:T(8,128)(2,1)S(1)} %shard_map.103), channel_id=1, source_target_pairs={{0,2},{2,4},{4,6},{6,0},{1,3},{3,5},{5,7},{7,1},{8,10},{10,12},{12... | collective-permute-start | bytes 1044488 | tf_op jit(solution)/shard_map/ppermute | solution.py:444
  64.5 0.3 collective-permute-start.6
  64.8 2.9 %collective-permute-start.7 = (bf16[128,1280]{1,0:T(8,128)(2,1)S(1)}, bf16[128,1280]{1,0:T(8,128)(2,1)S(1)}, u32[]{:S(2)}, u32[]{:S(2)}) collective-permute-start(bf16[128,1280]{1,0:T(8,128)(2,1)S(1)} %shard_map.101), channel_id=1, source_target_pairs={{0,2},{2,4},{4,6},{6,0},{1,3},{3,5},{5,7},{7,1},{8,10},{10,12},{12... | collective-permute-start | bytes 983048 | tf_op jit(solution)/shard_map/ppermute | solution.py:443
  67.7 0.0 collective-permute-done.8.refs_0_
  67.7 0.1 shard_map.104
  67.9 0.1 collective-permute-start.9
  67.9 11.3 %collective-permute-done.7.rb_ref = bf16[128,1280]{1,0:T(8,128)(2,1)S(1)} collective-permute-done((bf16[128,1280]{1,0:T(8,128)(2,1)S(1)}, bf16[128,1280]{1,0:T(8,128)(2,1)S(1)}, u32[]{:S(2)}, u32[]{:S(2)}) %collective-permute-start.7) | collective-permute-done | bytes 327712 | tf_op jit(solution)/shard_map/ppermute | solution.py:443
  79.2 2.6 %collective-permute-done.9.lb_ref = bf16[128,1280]{1,0:T(8,128)(2,1)S(1)} collective-permute-done((bf16[128,1280]{1,0:T(8,128)(2,1)S(1)}, bf16[128,1280]{1,0:T(8,128)(2,1)S(1)}, u32[]{:S(2)}, u32[]{:S(2)}) %collective-permute-start.9) | collective-permute-done | bytes 327712 | tf_op jit(solution)/shard_map/ppermute | solution.py:444
  81.8 0.0 collective-permute-done.5.ra_ref
  81.8 0.0 collective-permute-done.6.la_ref
  81.8 1.8 %finish.1 = bf16[128,2560]{1,0:T(8,128)(2,1)} custom-call(f32[8,128]{1,0:T(8,128)S(1)} %get-tuple-element.43.square_ref.refs_0_, f32[384,1280]{1,0:T(8,128)S(1)} %get-tuple-element.57.keep_ref.ka_ref, f32[384,1280]{1,0:T(8,128)S(1)} %get-tuple-element.58.keep_ref.kb_ref, bf16[408,1280]{1,0:T(8,128)(2,1)S(1)} %collective-permute-done.2.got_ref.ga_ref, ...), custom_call_target="tpu_custom_call" | custom-call | tf_op jit(solution)/shard_map/finish/pallas_call | solution.py:394
  (1 shorter events, 0.0 us)
Async XLA Ops:
  0.0 31.0 %copy-start.1 = (bf16[640]{0:T(1024)(128)(2,1)S(1)}, bf16[640]{0:T(1024)(128)(2,1)}, u32[]{:S(2)}) copy-start(bf16[640]{0:T(1024)(128)(2,1)} %param.16) | copy-start | bytes 3844
  0.0 31.0 %copy-start.2 = (f32[10]{0:T(128)S(1)}, f32[10]{0:T(128)}, u32[]{:S(2)}) copy-start(f32[10]{0:T(128)} %param.15) | copy-start | bytes 124
  27.1 14.8 %all-to-all-start.1 = ((bf16[32,4,640]{2,1,0:T(4,128)(2,1)}), bf16[32,4,640]{2,1,0:T(4,128)(2,1)S(1)}, u32[]{:S(2)}, u32[]{:S(2)}) async-start(bf16[32,4,640]{2,1,0:T(4,128)(2,1)} %shard_map.92), calls=%async_computation.1 | async-start | bytes 327680 | tf_op jit(solution)/shard_map/all_to_all | solution.py:422
  31.3 10.7 %copy-start = (bf16[1024,128]{1,0:T(8,128)(2,1)S(1)}, bf16[1024,128]{1,0:T(8,128)(2,1)}, u32[]{:S(2)}) copy-start(bf16[1024,128]{1,0:T(8,128)(2,1)} %c_ref.5) | copy-start | bytes 786436
  45.5 2.7 %collective-permute-start = (bf16[136,1280]{1,0:T(8,128)(2,1)S(1)}, bf16[136,1280]{1,0:T(8,128)(2,1)S(1)}, u32[]{:S(2)}, u32[]{:S(2)}) collective-permute-start(bf16[136,1280]{1,0:T(8,128)(2,1)S(1)} %get-tuple-element.38), channel_id=1, source_target_pairs={{0,1},{1,0},{2,3},{3,2},{4,5},{5,4},{6,7},{7,6},{8,9},{9,8},{10,11... | collective-permute-start | bytes 1044488 | tf_op jit(solution)/shard_map/ppermute | solution.py:427
  46.3 2.0 %collective-permute-start.1 = (bf16[128,1280]{1,0:T(8,128)(2,1)S(1)}, bf16[128,1280]{1,0:T(8,128)(2,1)S(1)}, u32[]{:S(2)}, u32[]{:S(2)}) collective-permute-start(bf16[128,1280]{1,0:T(8,128)(2,1)S(1)} %get-tuple-element.41), channel_id=1, source_target_pairs={{0,1},{1,0},{2,3},{3,2},{4,5},{5,4},{6,7},{7,6},{8,9},{9,8},{10,11... | collective-permute-start | bytes 983048 | tf_op jit(solution)/shard_map/ppermute | solution.py:429
  51.8 4.2 %collective-permute-start.2 = (bf16[408,1280]{1,0:T(8,128)(2,1)S(1)}, bf16[408,1280]{1,0:T(8,128)(2,1)S(1)}, u32[]{:S(2)}, u32[]{:S(2)}) collective-permute-start(bf16[408,1280]{1,0:T(8,128)(2,1)S(1)} %get-tuple-element.54), channel_id=1, source_target_pairs={{0,1},{1,0},{2,3},{3,2},{4,5},{5,4},{6,7},{7,6},{8,9},{9,8},{10,11... | collective-permute-start | bytes 3133448 | tf_op jit(solution)/shard_map/ppermute | solution.py:438
  52.0 3.9 %collective-permute-start.3 = (bf16[384,1280]{1,0:T(8,128)(2,1)S(1)}, bf16[384,1280]{1,0:T(8,128)(2,1)S(1)}, u32[]{:S(2)}, u32[]{:S(2)}) collective-permute-start(bf16[384,1280]{1,0:T(8,128)(2,1)S(1)} %get-tuple-element.50), channel_id=1, source_target_pairs={{0,1},{1,0},{2,3},{3,2},{4,5},{5,4},{6,7},{7,6},{8,9},{9,8},{10,11... | collective-permute-start | bytes 2949128 | tf_op jit(solution)/shard_map/ppermute | solution.py:436
  52.4 10.2 %collective-permute-start.4 = (bf16[136,1280]{1,0:T(8,128)(2,1)S(1)}, bf16[136,1280]{1,0:T(8,128)(2,1)S(1)}, u32[]{:S(2)}, u32[]{:S(2)}) collective-permute-start(bf16[136,1280]{1,0:T(8,128)(2,1)S(1)} %shard_map.97), channel_id=1, source_target_pairs={{0,2},{2,4},{4,6},{6,0},{1,3},{3,5},{5,7},{7,1},{8,10},{10,12},{12... | collective-permute-start | bytes 1044488 | tf_op jit(solution)/shard_map/ppermute | solution.py:434
  52.9 14.9 %collective-permute-start.8 = (bf16[128,1280]{1,0:T(8,128)(2,1)S(1)}, bf16[128,1280]{1,0:T(8,128)(2,1)S(1)}, u32[]{:S(2)}, u32[]{:S(2)}) collective-permute-start(bf16[128,1280]{1,0:T(8,128)(2,1)S(1)} %shard_map.98), channel_id=1, source_target_pairs={{0,6},{2,0},{4,2},{6,4},{1,7},{3,1},{5,3},{7,5},{8,14},{10,8},{12,... | collective-permute-start | bytes 983048 | tf_op jit(solution)/shard_map/ppermute | solution.py:434
  62.7 19.1 %collective-permute-start.5 = (bf16[136,1280]{1,0:T(8,128)(2,1)S(1)}, bf16[136,1280]{1,0:T(8,128)(2,1)S(1)}, u32[]{:S(2)}, u32[]{:S(2)}) collective-permute-start(bf16[136,1280]{1,0:T(8,128)(2,1)S(1)} %shard_map.103), channel_id=1, source_target_pairs={{0,2},{2,4},{4,6},{6,0},{1,3},{3,5},{5,7},{7,1},{8,10},{10,12},{12... | collective-permute-start | bytes 1044488 | tf_op jit(solution)/shard_map/ppermute | solution.py:444
  64.5 17.3 %collective-permute-start.6 = (bf16[136,1280]{1,0:T(8,128)(2,1)S(1)}, bf16[136,1280]{1,0:T(8,128)(2,1)S(1)}, u32[]{:S(2)}, u32[]{:S(2)}) collective-permute-start(bf16[136,1280]{1,0:T(8,128)(2,1)S(1)} %shard_map.102), channel_id=1, source_target_pairs={{0,6},{2,0},{4,2},{6,4},{1,7},{3,1},{5,3},{7,5},{8,14},{10,8},{12,... | collective-permute-start | bytes 1044488 | tf_op jit(solution)/shard_map/ppermute | solution.py:443
  64.8 14.4 %collective-permute-start.7 = (bf16[128,1280]{1,0:T(8,128)(2,1)S(1)}, bf16[128,1280]{1,0:T(8,128)(2,1)S(1)}, u32[]{:S(2)}, u32[]{:S(2)}) collective-permute-start(bf16[128,1280]{1,0:T(8,128)(2,1)S(1)} %shard_map.101), channel_id=1, source_target_pairs={{0,2},{2,4},{4,6},{6,0},{1,3},{3,5},{5,7},{7,1},{8,10},{10,12},{12... | collective-permute-start | bytes 983048 | tf_op jit(solution)/shard_map/ppermute | solution.py:443
  67.9 14.0 %collective-permute-start.9 = (bf16[128,1280]{1,0:T(8,128)(2,1)S(1)}, bf16[128,1280]{1,0:T(8,128)(2,1)S(1)}, u32[]{:S(2)}, u32[]{:S(2)}) collective-permute-start(bf16[128,1280]{1,0:T(8,128)(2,1)S(1)} %shard_map.104), channel_id=1, source_target_pairs={{0,6},{2,0},{4,2},{6,4},{1,7},{3,1},{5,3},{7,5},{8,14},{10,8},{12,... | collective-permute-start | bytes 983048 | tf_op jit(solution)/shard_map/ppermute | solution.py:444
where the time goes:
time: 83.9 us; the launch traced here: 83.6 us
  waiting for transfers between devices  25.1 us (30%)
  Pallas kernels  22.9 us (27%)
  blocking collectives  22.9 us (27%)
  starting transfers between devices  12.2 us (15%)
    all_to_all x1, blocking collectives, body(): lax.all_to_all(msg, ('z', 'y'), split_axis=0, concat_axis=0, tiled=True)  22.9 us
    pallas_call x14, Pallas kernels, local_call(): pl.pallas_call(kernel, in_specs=in_specs, out_specs=out_specs, out_shape=...  13.7 us
    ppermute x1, waiting for transfers between devices, body(): lax.ppermute(right_b, 'x', up)  11.3 us
    pallas_call x1, Pallas kernels, local_part(): pl.pallas_call(local_kernel, grid=(NBLK,), in_specs=[rows(CH), rows(CH),...  7.47 us
    ppermute x1, waiting for transfers between devices, body(): lax.ppermute(far_a, 'x', up)  6.5 us
    all_to_all x1, starting transfers between devices, body(): lax.all_to_all(seq_prefix(msg), ('z', 'y'), split_axis=0, concat_axis=0,...  3.87 us
    all_to_all x1, waiting for transfers between devices, body(): lax.all_to_all(seq_prefix(msg), ('z', 'y'), split_axis=0, concat_axis=0,...  3.19 us
    ppermute x1, starting transfers between devices, body(): lax.ppermute(right_b, 'x', up)  2.9 us
  transfers between devices with their start and end apart: 11, of which 5 were waited for; matrix products, arithmetic and copies ran while one was open for 0% of the time, Pallas kernels for 12%

commit v1 on v0

--- a/solution.py
+++ b/solution.py
@@ -20,7 +20,10 @@
 SEQ_DEV = 32
 PIECE = STATE // SEQ_DEV
 D = 2560
-DH = D // 2
+WA = 1408
+WB = D - WA
+CHUNKS = 8
+TILES = WA // HALF * (HALF // 8) + 1
 PADH = 16
 TALL = HALF + 8
 LOG2E = 1.4426950408889634
@@ -105,7 +108,7 @@
         msg_ref[q, :, CH : CH + HALF] = decays
 
 
-def prefix_kernel(msg_ref, out_ref, dec_ref):
+def prefix_kernel(msg_ref, out_hbm, dec_ref, out_ref, sem):
     for i in range(SEQ_DEV):
         for part in range(3):
             dec_ref[part, i : i + 1, :] = msg_ref[i, :, CH : CH + HALF].astype(F32)[part : part + 1]
@@ -117,16 +120,30 @@
         logs = logs + jnp.dot(dec_ref[part].astype(BF16), matrix, preferred_element_type=F32)
     decay = jnp.exp(logs)
     running = jnp.zeros((PIECE, CH), F32)
+    group = SEQ_DEV // CHUNKS
+    copies = []
     for i in range(SEQ_DEV):
         out_ref[i] = running.astype(BF16)
         running = decay[i : i + 1, :] * running + msg_ref[i, :, 0:CH].astype(F32)
-
-
-def local_kernel(x_ref, g_ref, b_ref, c_ref, dt_ref, ld_ref, skip_ref, gl_ref, fs_ref, run_ref, lead_ref, pad_ref, dtp_ref):
+        if i % group == group - 1:
+            span = pl.ds(i + 1 - group, group)
+            copies.append(pltpu.make_async_copy(out_ref.at[span], out_hbm.at[span], sem.at[i // group]))
+            copies[-1].start()
+    for copy in copies:
+        copy.wait()
+
+
+def local_kernel(
+    idx_ref, x_ref, g_ref, b_ref, c_ref, dt_ref, ld_ref, skip_ref, w_hbm, far_gl_ref, far_fs_ref, left_gl_ref, left_fs_ref,
+    right_gl_ref, right_fs_ref, own_gl_ref, own_fs_ref, w_ref,
+    gl_ref, fs_ref, run_ref, lead_ref, pad_ref, dtp_ref, sem
+):
     k = pl.program_id(0)
+    fetch = pltpu.make_async_copy(w_hbm.at[:, pl.ds(0, WA)], w_ref, sem.at[0])
 
     @pl.when(k == 0)
     def _():
+        fetch.start()
         run_ref[...] = jnp.zeros_like(run_ref)
         lead_ref[...] = jnp.zeros_like(lead_ref)
         pad_ref[...] = jnp.zeros_like(pad_ref)
@@ -183,9 +200,25 @@
             )
             gate = g_ref[span, lanes].astype(F32)
             gate = gate / (1.0 + jnp.exp(-gate))
-            out_rows = pl.ds(pl.multiple_of(k * BLOCK + HALF * r, HALF), HALF)
-            gl_ref[out_rows, lanes] = (mixed * gate).astype(BF16)
-            fs_ref[out_rows, lanes] = (grown[span, lanes] * lead[:, lanes] * gate).astype(BF16)
+            gl_ref[span, lanes] = (mixed * gate).astype(BF16)
+            fs_ref[span, lanes] = (grown[span, lanes] * lead[:, lanes] * gate).astype(BF16)
+
+    roles = (
+        (far_gl_ref, far_fs_ref),
+        (left_gl_ref, left_fs_ref),
+        (right_gl_ref, right_fs_ref),
+        (own_gl_ref, own_fs_ref),
+    )
+    for role, (to_gl_ref, to_fs_ref) in enumerate(roles):
+
+        @pl.when(k == idx_ref[1 + role])
+        def _():
+            to_gl_ref[...] = gl_ref[...]
+            to_fs_ref[...] = fs_ref[...]
+
+    @pl.when(k == NBLK - 1)
+    def _():
+        fetch.wait()
 
 
 def square_rows(total):
@@ -197,104 +230,118 @@
     return jnp.sum(ref[first : first + 8, 0:HALF].astype(F32), axis=0, keepdims=True)
 
 
-def gate_kernel(first, count, idx_ref, p_ref, gain_ref, c_ref, gl_ref, fs_ref, *rest):
-    fetch = None
-    if len(rest) > 2:
-        w_hbm, rows_ref, square_ref, p_out_ref, w_ref, st_ref, sem = rest
-        fetch = pltpu.make_async_copy(w_hbm.at[:, 0:DH], w_ref, sem.at[0])
-        fetch.start()
+def gate_block(place, idx_ref, state, gain, c_ref, gl_ref, fs_ref, rows_ref, square_ref):
+    squares = []
+    for n, half in enumerate((1 - idx_ref[0], idx_ref[0])):
+        there = pl.ds(pl.multiple_of((2 * idx_ref[place] + half) * HALF, HALF), HALF)
+        here = pl.ds(pl.multiple_of(half * HALF, HALF), HALF)
+        gated = gl_ref[here, :].astype(F32) + fs_ref[here, :].astype(F32) * jnp.dot(
+            c_ref[there, :], state, preferred_element_type=F32
+        )
+        sums = jnp.sum(gated * gated, axis=1, keepdims=True)
+        squares.append(jnp.transpose(jnp.broadcast_to(sums, (HALF, HALF)))[0:1, :])
+        rows_ref[HALF * n : HALF * (n + 1), :] = (gated * gain).astype(BF16)
+    square_ref[...] = jnp.concatenate(squares + [jnp.zeros((8 - len(squares), HALF), F32)], axis=0)
+
+
+def gate_kernel(place, idx_ref, p_ref, gain_ref, c_ref, gl_ref, fs_ref, rows_ref, square_ref, *rest):
+    if rest:
+        p_out_ref, st_ref = rest
         for q in range(SEQ_DEV):
             st_ref[PIECE * q : PIECE * (q + 1), :] = p_ref[q].astype(F32)
         state = st_ref[...].astype(BF16)
         p_out_ref[...] = state
     else:
-        rows_ref, square_ref = rest
         state = p_ref[...]
-    gain = gain_ref[...]
-    squares = []
-    for side, half in enumerate((1 - idx_ref[0], idx_ref[0])):
-        for i in range(count):
-            rows = pl.ds(pl.multiple_of((2 * idx_ref[first + i] + half) * HALF, HALF), HALF)
-            gated = gl_ref[rows, :].astype(F32) + fs_ref[rows, :].astype(F32) * jnp.dot(
-                c_ref[rows, :], state, preferred_element_type=F32
-            )
-            sums = jnp.sum(gated * gated, axis=1, keepdims=True)
-            squares.append(jnp.transpose(jnp.broadcast_to(sums, (HALF, HALF)))[0:1, :])
-            place = count * side + i
-            rows_ref[HALF * place : HALF * (place + 1), :] = (gated * gain).astype(BF16)
-    square_ref[...] = jnp.concatenate(squares + [jnp.zeros((8 - len(squares), HALF), F32)], axis=0)
-    if fetch is not None:
-        fetch.wait()
-
-
-def put_squares(ref, base, total):
-    ref[base : base + TALL - HALF, 0:HALF] = square_rows(total)
-    ref[base : base + TALL - HALF, HALF:DH] = jnp.zeros((TALL - HALF, DH - HALF), BF16)
-
-
-def product_kernel(rows_ref, square_ref, w_ref, *rest):
-    fetch = None
-    if len(rest) > 2:
-        w_hbm, send_ref, keep_ref, w_next_ref, sem = rest
-        fetch = pltpu.make_async_copy(w_hbm.at[:, DH:D], w_next_ref, sem.at[0])
+    gate_block(place, idx_ref, state, gain_ref[...], c_ref, gl_ref, fs_ref, rows_ref, square_ref)
+
+
+def product_kernel(rows_ref, square_ref, w_ref, send_ref, keep_ref):
+    width = keep_ref.shape[1]
+    rows = rows_ref[...]
+    for base in range(0, width, BLOCK):
+        cols = slice(base, min(base + BLOCK, width))
+        value = jnp.dot(rows, w_ref[:, cols], preferred_element_type=F32)
+        keep_ref[:, cols] = value[HALF:BLOCK]
+        send_ref[0:HALF, cols] = value[0:HALF].astype(BF16)
+    if send_ref.shape[0] == TALL:
+        send_ref[HALF:TALL, 0:HALF] = square_rows(square_ref[0:1, :])
+        send_ref[HALF:TALL, HALF:width] = jnp.zeros((TALL - HALF, width - HALF), BF16)
+
+
+def middle_kernel(
+    idx_ref, p_ref, gain_ref, c_ref, left_gl_ref, left_fs_ref, far_rows_ref, far_square_ref, right_gl_hbm, right_fs_hbm, w_hbm,
+    send_ref, keep_ref, left_rows_ref, left_square_ref, right_rows_ref, right_square_ref, w_ref,
+    right_gl_ref, right_fs_ref, sem
+):
+    fetches = [
+        pltpu.make_async_copy(right_gl_hbm, right_gl_ref, sem.at[0]),
+        pltpu.make_async_copy(right_fs_hbm, right_fs_ref, sem.at[1]),
+        pltpu.make_async_copy(w_hbm.at[:, pl.ds(WA, WB)], w_ref, sem.at[2]),
+    ]
+    for fetch in fetches:
         fetch.start()
-    else:
-        send_ref, keep_ref = rest
-    count = rows_ref.shape[0] // (2 * HALF)
-    tall = send_ref.shape[0] // count
-    rows = rows_ref[...]
-    for j in range(DH // BLOCK):
-        cols = slice(BLOCK * j, BLOCK * (j + 1))
-        value = jnp.dot(rows, w_ref[:, cols], preferred_element_type=F32)
-        keep_ref[:, cols] = value[HALF * count : 2 * HALF * count]
-        for i in range(count):
-            send_ref[tall * i : tall * i + HALF, cols] = value[HALF * i : HALF * (i + 1)].astype(BF16)
-    if tall == TALL:
-        for i in range(count):
-            put_squares(send_ref, tall * i + HALF, square_ref[i : i + 1, :])
-    if fetch is not None:
-        fetch.wait()
-
-
-def join_kernel(place, keep_ref, got_ref, *refs):
+    state, gain = p_ref[...], gain_ref[...]
+    gate_block(2, idx_ref, state, gain, c_ref, left_gl_ref, left_fs_ref, left_rows_ref, left_square_ref)
+    fetches[0].wait()
+    fetches[1].wait()
+    gate_block(3, idx_ref, state, gain, c_ref, right_gl_ref, right_fs_ref, right_rows_ref, right_square_ref)
+    fetches[2].wait()
+    product_kernel(far_rows_ref, far_square_ref, w_ref, send_ref, keep_ref)
+
+
+def tiles_of(width):
+    per_row = width // HALF
+    for n in range(HALF // 8 * per_row):
+        yield n, n // per_row * 8, slice(n % per_row * HALF, (n % per_row + 1) * HALF)
+
+
+def join_kernel(keep_ref, got_ref, *refs):
     out_ref = refs[-1]
-    count = keep_ref.shape[0] // HALF
-    tall = got_ref.shape[0] // count
-    value = keep_ref[HALF * place : HALF * (place + 1), :] + got_ref[tall * place : tall * place + HALF, :].astype(F32)
-    squares = tall == TALL
-    more = refs[squares:-1]
+    if got_ref.shape[0] == HALF:
+        value = keep_ref[...] + got_ref[...].astype(F32)
+        for ref in refs[:-1]:
+            value = value + ref[...].astype(F32)
+        out_ref[...] = value.astype(BF16)
+        return
+    square_ref, more = refs[0], refs[1:-1]
+    for n, row, lanes in tiles_of(keep_ref.shape[1]):
+        value = keep_ref[row : row + 8, lanes] + got_ref[row : row + 8, lanes].astype(F32)
+        for ref in more:
+            value = value + ref[n].astype(F32)
+        out_ref[n] = value.astype(BF16)
+    total = square_ref[1:2, :] + squares_of(got_ref, HALF)
     for ref in more:
-        value = value + ref[0:HALF, :].astype(F32)
-    out_ref[0:HALF, :] = value.astype(BF16)
-    if squares:
-        total = refs[0][count + place : count + place + 1, :] + squares_of(got_ref, tall * place + HALF)
-        for ref in more:
-            total = total + squares_of(ref, HALF)
-        put_squares(out_ref, HALF, total)
-
-
-def finish_kernel(devices, square_ref, ka_ref, kb_ref, ga_ref, gb_ref, ra_ref, la_ref, rb_ref, lb_ref, out_ref, scale_ref):
-    rows = out_ref.shape[0]
-    count = ka_ref.shape[0] // HALF
-    last = count - 1
-
-    @pl.when(pl.program_id(0) == 0)
-    def _():
-        total = square_ref[count + last : count + last + 1, :] + squares_of(ga_ref, TALL * last + HALF)
-        total = total + squares_of(ra_ref, HALF) + squares_of(la_ref, HALF)
-        scale = lax.rsqrt(total / (CH * devices) + 1e-05)
-        scale_ref[...] = jnp.transpose(jnp.broadcast_to(scale, (HALF, HALF)))
-
-    def part(ref, tall):
-        return ref[pl.ds(pl.multiple_of(pl.program_id(0) * rows + tall * last, 8), rows), :].astype(F32)
-
-    span = pl.ds(pl.multiple_of(pl.program_id(0) * rows, rows), rows)
-    scale = scale_ref[span, 0:1]
-    for i, (keep, got, tall, one, two) in enumerate(
-        ((ka_ref, ga_ref, TALL, ra_ref, la_ref), (kb_ref, gb_ref, HALF, rb_ref, lb_ref))
-    ):
-        value = part(keep, HALF) + part(got, tall) + one[span, :].astype(F32) + two[span, :].astype(F32)
-        out_ref[:, DH * i : DH * (i + 1)] = (value * scale).astype(BF16)
+        total = total + last_squares(ref)
+    out_ref[TILES - 1] = square_rows(total)
+
+
+def last_squares(ref):
+    return jnp.sum(ref[TILES - 1].astype(F32), axis=0, keepdims=True)
+
+
+def finish_kernel(
+    devices, square_ref, ka_ref, kb_ref, ga_ref, gb_ref, ra_ref, la_ref, rb_ref, lb_ref, out_hbm, scale_ref, out_ref, sem
+):
+    total = square_ref[1:2, :] + squares_of(ga_ref, HALF) + last_squares(ra_ref) + last_squares(la_ref)
+    scale = lax.rsqrt(total / (CH * devices) + 1e-05)
+    scale_ref[...] = jnp.transpose(jnp.broadcast_to(scale, (HALF, HALF)))
+    copies = []
+    group = HALF // CHUNKS
+    for n, row, lanes in tiles_of(WA):
+        span = slice(row, row + 8)
+        value = ka_ref[span, lanes] + ga_ref[span, lanes].astype(F32) + ra_ref[n].astype(F32) + la_ref[n].astype(F32)
+        out_ref[span, lanes] = (value * scale_ref[span, 0:1]).astype(BF16)
+        if lanes.stop == WA and (row + 8) % group == 0:
+            span = slice(row + 8 - group, row + 8)
+            value = kb_ref[span, :] + gb_ref[span, :].astype(F32) + rb_ref[span, :].astype(F32)
+            value = value + lb_ref[span, :].astype(F32)
+            out_ref[span, WA:D] = (value * scale_ref[span, 0:1]).astype(BF16)
+            span = pl.ds(row + 8 - group, group)
+            copies.append(pltpu.make_async_copy(out_ref.at[span, :], out_hbm.at[span, :], sem.at[len(copies)]))
+            copies[-1].start()
+    for copy in copies:
+        copy.wait()
 
 
 VMEM = pl.BlockSpec(memory_space=pltpu.VMEM)
@@ -336,71 +383,76 @@
 
 def seq_prefix(msg):
     outs = (((SEQ_DEV, PIECE, CH), BF16),)
-    scratch = [((3, SEQ_DEV, HALF), F32)]
-    return local_call(prefix_kernel, (msg,), outs, scratch)[0]
+    scratch = [((3, SEQ_DEV, HALF), F32), outs[0], CHUNKS]
+    return local_call(prefix_kernel, (msg,), outs, scratch, out_specs=[HBM])[0]
 
 
 def whole(shape):
     return pl.BlockSpec(shape, lambda *_: (0,) * len(shape))
 
 
-def local_part(x, g, b, c, dt, ld, skip):
+def local_part(order, x, g, b, c, dt, ld, skip, w):
     rows = lambda width: pl.BlockSpec((BLOCK, width), lambda k: (k, 0))
     heads = pl.BlockSpec((HEADS, BLOCK), lambda k: (0, k))
+    there = lambda v: pltpu.with_memory_space_constraint(v, pltpu.HBM)
     return pl.pallas_call(
         local_kernel,
         grid=(NBLK,),
-        in_specs=[rows(CH), rows(CH), rows(STATE), rows(STATE), heads, heads, whole((1, CH))],
-        out_specs=(VMEM, VMEM),
-        out_shape=(jax.ShapeDtypeStruct((ROWS, CH), BF16), jax.ShapeDtypeStruct((ROWS, CH), BF16)),
+        in_specs=[SMEM, rows(CH), rows(CH), rows(STATE), rows(STATE), heads, heads, whole((1, CH)), HBM],
+        out_specs=(VMEM,) * 4 + (whole((BLOCK, CH)),) * 4 + (VMEM,),
+        out_shape=(jax.ShapeDtypeStruct((BLOCK, CH), BF16),) * 4
+        + (pltpu.HBM((BLOCK, CH), BF16),) * 4
+        + (jax.ShapeDtypeStruct((CH, WA), BF16),),
         scratch_shapes=[
+            pltpu.VMEM((BLOCK, CH), BF16),
+            pltpu.VMEM((BLOCK, CH), BF16),
             pltpu.VMEM((STATE, CH), F32),
             pltpu.VMEM((PADH, HALF), F32),
             pltpu.VMEM((PADH, BLOCK), F32),
             pltpu.VMEM((PADH, BLOCK), F32),
+            pltpu.SemaphoreType.DMA((1,)),
         ],
         cost_estimate=pl.CostEstimate(flops=int(3e9), bytes_accessed=0, transcendentals=0),
         compiler_params=pltpu.CompilerParams(vmem_limit_bytes=LIMIT),
         name="local_part",
-    )(*(pltpu.with_memory_space_constraint(v, pltpu.HBM) for v in (x, g, b, c, dt, ld)), skip)
-
-
-def gated_rows(order, first, count, prefix, gain, c, gl, fs, *w):
-    outs = [((2 * HALF * count, CH), BF16), ((8, HALF), F32)]
+    )(order, *(there(v) for v in (x, g, b, c, dt, ld)), skip, there(w))
+
+
+def gated_rows(order, place, prefix, *args):
+    outs = [((BLOCK, CH), BF16), ((8, HALF), F32)]
     scratch = []
-    in_specs = [SMEM] + [VMEM] * 5 + [HBM] * len(w)
-    if w:
-        outs += [((STATE, CH), BF16), ((CH, DH), BF16)]
-        scratch = [((STATE, CH), F32), 1]
-    kernel = functools.partial(gate_kernel, first, count)
-    return local_call(kernel, (order, prefix, gain, c, gl, fs, *w), outs, scratch, 5e8 * count, in_specs)
-
-
-def product(rows, squares, w, tall, *w_next):
-    count = rows.shape[0] // (2 * HALF)
-    outs = [((tall * count, DH), BF16), ((HALF * count, DH), F32)] + [((CH, DH), BF16)] * len(w_next)
-    in_specs = [VMEM] * 3 + [HBM] * len(w_next)
-    flops = 2 * rows.shape[0] * CH * DH
-    return local_call(product_kernel, (rows, squares, w, *w_next), outs, [1] * len(w_next), flops, in_specs)
-
-
-def join(place, keep, got, *more):
-    tall = got.shape[0] * HALF // keep.shape[0]
-    return local_call(functools.partial(join_kernel, place), (keep, got, *more), (((tall, DH), BF16),))[0]
+    if prefix.ndim == 3:
+        outs.append(((STATE, CH), BF16))
+        scratch.append(((STATE, CH), F32))
+    kernel = functools.partial(gate_kernel, place)
+    return local_call(kernel, (order, prefix, *args), outs, scratch, 5e8, [SMEM] + [VMEM] * 5)
+
+
+def product(rows, squares, w):
+    width = w.shape[1]
+    tall = TALL if width == WA else HALF
+    outs = [((tall, width), BF16), ((HALF, width), F32)]
+    return local_call(product_kernel, (rows, squares, w), outs, (), 2 * BLOCK * CH * width)
+
+
+def middle(*args):
+    gated = [((BLOCK, CH), BF16), ((8, HALF), F32)]
+    outs = [((HALF, WB), BF16), ((HALF, WB), F32), *gated, *gated, ((CH, WB), BF16)]
+    scratch = [gated[0], gated[0], 3]
+    in_specs = [SMEM] + [VMEM] * 7 + [HBM] * 3
+    return local_call(middle_kernel, args, outs, scratch, 2e9, in_specs)
+
+
+def join(keep, got, *more):
+    out = (TILES, 8, HALF) if got.shape[0] == TALL else keep.shape
+    return local_call(join_kernel, (keep, got, *more), ((out, BF16),))[0]
 
 
 def finish(devices, *args):
-    rows = 32
-    return pl.pallas_call(
-        functools.partial(finish_kernel, devices),
-        grid=(HALF // rows,),
-        in_specs=[VMEM] * len(args),
-        out_specs=pl.BlockSpec((rows, D), lambda i: (i, 0)),
-        out_shape=jax.ShapeDtypeStruct((HALF, D), BF16),
-        scratch_shapes=[pltpu.VMEM((HALF, HALF), F32)],
-        compiler_params=pltpu.CompilerParams(vmem_limit_bytes=LIMIT),
-        name="finish",
-    )(*args)
+    kernel = functools.partial(finish_kernel, devices)
+    out = ((HALF, D), BF16)
+    scratch = [((HALF, HALF), F32), out, CHUNKS]
+    return local_call(kernel, args, (out,), scratch, out_specs=[HBM])[0]
 
 
 def after(value, earlier):
@@ -413,36 +465,49 @@
     up = [(i, (i + 1) % chips) for i in range(chips)]
     down = [(i, (i - 1) % chips) for i in range(chips)]
     swap = [(0, 1), (1, 0)]
-    far, right, left = (chip + 2) % chips, (chip + 1) % chips, (chip + 3) % chips
-    order = jnp.stack([core, far, right, left, chip]).astype(jnp.int32)
+    order = jnp.stack([core, (chip + 2) % chips, (chip + 3) % chips, (chip + 1) % chips, chip]).astype(jnp.int32)
     msg = local_state(x, b, dt.T, ld.T)
     msg = lax.all_to_all(msg, ("z", "y"), split_axis=0, concat_axis=0, tiled=True)
     skip_wide = jnp.repeat(skip, WIDTH)[None, :]
-    gl, fs = local_part(x, g, b, c, dt.T, ld.T, skip_wide)
+    *parts_of, w_a = local_part(order, x, g, b, c, dt.T, ld.T, skip_wide, w)
+    far, left, right, own = (parts_of[2 * i : 2 * i + 2] for i in range(4))
     prefix = lax.all_to_all(seq_prefix(msg), ("z", "y"), split_axis=0, concat_axis=0, tiled=True)
     gain_row = gain.astype(F32)[None, :]
 
-    rows0, square0, prefix, w_a = gated_rows(order, 1, 1, prefix, gain_row, c, gl, fs, w)
-    send_a, keep_a, w_b = product(rows0, square0, w_a, TALL, w)
-    got_a = lax.ppermute(send_a, "c", swap)
-    send_b, keep_b = product(after(rows0, send_a), square0, w_b, HALF)
-    got_b = lax.ppermute(send_b, "c", swap)
-    rows1, square1 = gated_rows(order, 2, 3, after(prefix, send_b), gain_row, c, gl, fs)
-    far_a = join(0, after(keep_a, rows1), got_a, square0)
-    far_b = join(0, after(keep_b, far_a), got_b)
-    rows1 = after(rows1, far_b)
+    rows, square, prefix = gated_rows(order, 1, prefix, gain_row, c, *far)
+    send, far_keep_a = product(rows, square, w_a)
+    far_got_a = lax.ppermute(send, "c", swap)
+    send, far_keep_b, rows_left, square_left, rows_right, square_right, w_b = middle(
+        order, prefix, gain_row, c, *left, after(rows, send), square, *right, w
+    )
+    far_got_b = lax.ppermute(send, "c", swap)
+    far_a = join(after(far_keep_a, send), far_got_a, square)
+    last = far_b = join(after(far_keep_b, far_a), far_got_b)
     far_a, far_b = lax.ppermute(far_a, "x", up), lax.ppermute(far_b, "x", down)
-    send_b, keep_b = product(rows1, square1, w_b, HALF)
-    got_b = lax.ppermute(send_b, "c", swap)
-    send_a, keep_a = product(after(rows1, send_b), square1, w_a, TALL)
-    got_a = lax.ppermute(send_a, "c", swap)
-    right_b = join(0, after(keep_b, send_a), got_b)
-    left_a = join(1, after(keep_a, right_b), got_a, square1)
-    right_a = join(0, after(keep_a, left_a), got_a, square1, far_a)
-    left_b = join(1, after(keep_b, right_a), got_b, far_b)
-    right_b, left_a = lax.ppermute(right_b, "x", up), lax.ppermute(left_a, "x", down)
-    right_a, left_b = lax.ppermute(right_a, "x", up), lax.ppermute(left_b, "x", down)
-    return finish(2 * chips, square1, keep_a, keep_b, got_a, got_b, right_a, left_a, right_b, left_b)
+
+    send, left_keep_a = product(after(rows_left, last), square_left, w_a)
+    left_got_a = lax.ppermute(send, "c", swap)
+    send, right_keep_b = product(after(rows_right, send), square_right, w_b)
+    right_got_b = lax.ppermute(send, "c", swap)
+    last = left_a = join(after(left_keep_a, send), left_got_a, square_left)
+    left_a = lax.ppermute(left_a, "x", down)
+    last = right_b = join(after(right_keep_b, last), right_got_b)
+    right_b = lax.ppermute(right_b, "x", up)
+    send, right_keep_a = product(after(rows_right, last), square_right, w_a)
+    right_got_a = lax.ppermute(send, "c", swap)
+    send, left_keep_b = product(after(rows_left, send), square_left, w_b)
+    left_got_b = lax.ppermute(send, "c", swap)
+    last = right_a = join(after(right_keep_a, send), right_got_a, square_right, far_a)
+    right_a = lax.ppermute(right_a, "x", up)
+    last = left_b = join(after(left_keep_b, last), left_got_b, far_b)
+    left_b = lax.ppermute(left_b, "x", down)
+
+    rows, square = gated_rows(order, 4, after(prefix, last), gain_row, c, *own)
+    send, keep_a = product(rows, square, w_a)
+    got_a = lax.ppermute(send, "c", swap)
+    send, keep_b = product(after(rows, send), square, w_b)
+    got_b = lax.ppermute(send, "c", swap)
+    return finish(2 * chips, square, keep_a, keep_b, got_a, got_b, right_a, left_a, right_b, left_b)
 
 
 def solution(mesh):

time: 83.9 us -> 87.4 us (1.042)
  the two profiles are of different devices: /device:TPU:6 before, /device:TPU:1 now
where the time goes in v1:
time: 87.4 us; the launch traced here: 87.2 us
  Pallas kernels  24.7 us (28%)
  blocking collectives  21.8 us (25%)
  waiting for transfers between devices  21.1 us (24%)
  starting transfers between devices  19 us (22%)
    all_to_all x1, blocking collectives, body(): lax.all_to_all(msg, ('z', 'y'), split_axis=0, concat_axis=0, tiled=True)  21.8 us
    pallas_call x19, Pallas kernels, local_call(): pl.pallas_call(kernel, in_specs=in_specs, out_specs=out_specs, out_shape=...  16 us
    pallas_call x1, Pallas kernels, local_part(): pl.pallas_call(local_kernel, grid=(NBLK,), in_specs=[SMEM, rows(CH), rows...  8.65 us
    ppermute x1, waiting for transfers between devices, body(): lax.ppermute(far_a, 'x', up)  6.95 us
    ppermute x1, waiting for transfers between devices, body(): left_b = lax.ppermute(left_b, 'x', down)  6.32 us
    all_to_all x1, starting transfers between devices, body(): lax.all_to_all(seq_prefix(msg), ('z', 'y'), split_axis=0, concat_axis=0,...  4.62 us
    ppermute x1, waiting for transfers between devices, body(): left_a = lax.ppermute(left_a, 'x', down)  4.57 us
    ppermute x1, starting transfers between devices, body(): far_got_a = lax.ppermute(send, 'c', swap)  3.32 us
  transfers between devices with their start and end apart: 15, of which 7 were waited for; matrix products, arithmetic and copies ran while one was open for 0% of the time, Pallas kernels for 18%

profile of v1, /device:TPU:1, one launch (start us, length us, event | category | flops | bytes accessed | tf_op | source)
XLA Modules:
  0.0 87.2 jit_solution(9548111087114662635)
XLA Ops:
  0.0 3.2 %shard_map.91 = bf16[32,4,768]{2,1,0:T(4,128)(2,1)S(1)} custom-call(bf16[1024,640]{1,0:T(8,128)(2,1)} %x_ref.1, bf16[1024,128]{1,0:T(8,128)(2,1)} %b_ref.1, f32[10,1024]{1,0:T(8,128)} %bitcast.7, f32[10,1024]{1,0:T(8,128)} %bitcast.9), custom_call_target="tpu_custom_call" | custom-call | flops 1000000000 | tf_op jit(solution)/shard_map/pallas_call | solution.py:356
  3.2 21.8 %all_to_all.10.msg_ref = bf16[32,4,768]{2,1,0:T(4,128)(2,1)S(1)} all-to-all(bf16[32,4,768]{2,1,0:T(4,128)(2,1)S(1)} %shard_map.91), channel_id=1, replica_groups=mesh['z'=8,'y'=4,'x'=4,'c'=2] {'z','y'}, dimensions={0} | all-to-all | bytes 393216 | tf_op jit(solution)/shard_map/all_to_all | solution.py:470
  25.0 1.0 %shard_map.92 = bf16[32,4,640]{2,1,0:T(4,128)(2,1)} custom-call(bf16[32,4,768]{2,1,0:T(4,128)(2,1)S(1)} %all_to_all.10.msg_ref), custom_call_target="tpu_custom_call" | custom-call | flops 100000000 | tf_op jit(solution)/shard_map/pallas_call | solution.py:356
  26.0 4.6 %all-to-all-start.1 = ((bf16[32,4,640]{2,1,0:T(4,128)(2,1)}), bf16[32,4,640]{2,1,0:T(4,128)(2,1)S(1)}, u32[]{:S(2)}, u32[]{:S(2)}) async-start(bf16[32,4,640]{2,1,0:T(4,128)(2,1)} %shard_map.92), calls=%async_computation.1 | async-start | bytes 327680 | tf_op jit(solution)/shard_map/all_to_all | solution.py:474
  30.6 0.1 broadcast_in_dim.10
  30.7 0.1 broadcast_in_dim_reshape.3.skip_ref
  30.8 0.1 stack.23.idx_ref
  30.9 8.6 %local_part.1 = (bf16[256,640]{1,0:T(8,128)(2,1)S(1)}, bf16[256,640]{1,0:T(8,128)(2,1)S(1)}, bf16[256,640]{1,0:T(8,128)(2,1)S(1)}, bf16[256,640]{1,0:T(8,128)(2,...) custom-call(s32[5]{0:T(128)S(1)} %stack.23.idx_ref, ...), custom_call_target="tpu_custom_call" | custom-call | flops 3000000000 | tf_op jit(solution)/shard_map/local_part/pallas_call | solution.py:398
  39.5 0.7 all-to-all-done.1.p_ref
  40.2 1.0 %shard_map.93 = (bf16[256,640]{1,0:T(8,128)(2,1)S(1)}, f32[8,128]{1,0:T(8,128)S(1)}, bf16[128,640]{1,0:T(8,128)(2,1)S(1)}) custom-call(s32[5]{0:T(128)S(1)} %stack.23.idx_ref, bf16[32,4,640]{2,1,0:T(4,128)(2,1)S(1)} %all-to-all-done.1.p_ref, f32[1,640]{1,0:T(1,128)S(1)} %reshape.gain_ref, bf16[1024,128]{1,0:T(8,128)(2,1)S(1)} %copy-done, ...), custom_call_target="tpu_custom_call" | custom-call | flops 500000000 | tf_op jit(solution)/shard_map/pallas_call | solution.py:356
  41.2 0.8 shard_map.94
  42.0 3.3 %collective-permute-start = (bf16[136,1408]{1,0:T(8,128)(2,1)S(1)}, bf16[136,1408]{1,0:T(8,128)(2,1)S(1)}, u32[]{:S(2)}, u32[]{:S(2)}) collective-permute-start(bf16[136,1408]{1,0:T(8,128)(2,1)S(1)} %get-tuple-element.61), channel_id=1, source_target_pairs={{0,1},{1,0},{2,3},{3,2},{4,5},{5,4},{6,7},{7,6},{8,9},{9,8},{10,11... | collective-permute-start | bytes 1148936 | tf_op jit(solution)/shard_map/ppermute | solution.py:479
  45.3 3.1 %shard_map.95 = (bf16[128,1152]{1,0:T(8,128)(2,1)S(1)}, f32[128,1152]{1,0:T(8,128)S(1)}, bf16[256,640]{1,0:T(8,128)(2,1)S(1)}, f32[8,128]{1,0:T(8,128)S(1)}, bf1...) custom-call(s32[5]{0:T(128)S(1)} %stack.23.idx_ref, ...), custom_call_target="tpu_custom_call" | custom-call | flops 2000000000 | tf_op jit(solution)/shard_map/pallas_call | solution.py:356
  48.4 0.1 collective-permute-start.1
  48.6 0.1 shard_map.96
  48.6 1.5 %collective-permute-done.1.got_ref = bf16[128,1152]{1,0:T(8,128)(2,1)S(1)} collective-permute-done((bf16[128,1152]{1,0:T(8,128)(2,1)S(1)}, bf16[128,1152]{1,0:T(8,128)(2,1)S(1)}, u32[]{:S(2)}, u32[]{:S(2)}) %collective-permute-start.1) | collective-permute-done | bytes 294944 | tf_op jit(solution)/shard_map/ppermute | solution.py:483
  50.1 0.1 shard_map.97
  50.2 0.8 shard_map.98
  50.9 0.2 collective-permute-start.2
  51.2 0.7 shard_map.99
  51.8 0.5 collective-permute-start.3
  52.3 0.4 collective-permute-done.2.got_ref
  52.7 0.1 shard_map.100
  52.8 0.6 collective-permute-done.3.got_ref
  53.5 0.1 shard_map.101
  53.5 0.8 shard_map.102
  54.3 0.5 collective-permute-start.4
  54.8 1.2 %collective-permute-start.5 = (bf16[177,8,128]{2,1,0:T(8,128)(2,1)S(1)}, bf16[177,8,128]{2,1,0:T(8,128)(2,1)S(1)}, u32[]{:S(2)}, u32[]{:S(2)}) collective-permute-start(bf16[177,8,128]{2,1,0:T(8,128)(2,1)S(1)} %shard_map.96), channel_id=1, source_target_pairs={{0,2},{2,4},{4,6},{6,0},{1,3},{3,5},{5,7},{7,1},{8,10},{10,12},{12... | collective-permute-start | bytes 1087496 | tf_op jit(solution)/shard_map/ppermute | solution.py:486
  56.0 1.5 %collective-permute-start.7 = (bf16[128,1152]{1,0:T(8,128)(2,1)S(1)}, bf16[128,1152]{1,0:T(8,128)(2,1)S(1)}, u32[]{:S(2)}, u32[]{:S(2)}) collective-permute-start(bf16[128,1152]{1,0:T(8,128)(2,1)S(1)} %shard_map.97), channel_id=1, source_target_pairs={{0,6},{2,0},{4,2},{6,4},{1,7},{3,1},{5,3},{7,5},{8,14},{10,8},{12,... | collective-permute-start | bytes 884744 | tf_op jit(solution)/shard_map/ppermute | solution.py:486
  57.5 0.7 shard_map.103
  58.1 0.8 collective-permute-start.6
  58.9 0.0 collective-permute-start.12
  58.9 6.9 %collective-permute-done.5.refs_1_ = bf16[177,8,128]{2,1,0:T(8,128)(2,1)S(1)} collective-permute-done((bf16[177,8,128]{2,1,0:T(8,128)(2,1)S(1)}, bf16[177,8,128]{2,1,0:T(8,128)(2,1)S(1)}, u32[]{:S(2)}, u32[]{:S(2)}) %collective-permute-start.5) | collective-permute-done | bytes 362528 | tf_op jit(solution)/shard_map/ppermute | solution.py:486
  65.9 0.1 shard_map.104
  66.0 0.0 collective-permute-done.6.got_ref
  66.0 0.1 shard_map.105
  66.1 1.0 %shard_map.106 = (bf16[256,640]{1,0:T(8,128)(2,1)S(1)}, f32[8,128]{1,0:T(8,128)S(1)}) custom-call(s32[5]{0:T(128)S(1)} %stack.23.idx_ref, bf16[128,640]{1,0:T(8,128)(2,1)S(1)} %get-tuple-element.91.p_ref, f32[1,640]{1,0:T(1,128)S(1)} %reshape.gain_ref, bf16[1024,128]{1,0:T(8,128)(2,1)S(1)} %copy-done, bf16[256,640]{1,0:T(8,128)(2,1)S(1)} %copy-done.1, ...), custom_call_target="tpu_custom_call" | custom-call | flops 500000000 | tf_op jit(solution)/shard_map/pallas_call | solution.py:356
  67.1 0.8 shard_map.107
  67.9 1.7 %collective-permute-start.8 = (bf16[136,1408]{1,0:T(8,128)(2,1)S(1)}, bf16[136,1408]{1,0:T(8,128)(2,1)S(1)}, u32[]{:S(2)}, u32[]{:S(2)}) collective-permute-start(bf16[136,1408]{1,0:T(8,128)(2,1)S(1)} %get-tuple-element.97), channel_id=1, source_target_pairs={{0,1},{1,0},{2,3},{3,2},{4,5},{5,4},{6,7},{7,6},{8,9},{9,8},{10,11... | collective-permute-start | bytes 1148936 | tf_op jit(solution)/shard_map/ppermute | solution.py:507
  69.6 1.3 %collective-permute-start.11 = (bf16[177,8,128]{2,1,0:T(8,128)(2,1)S(1)}, bf16[177,8,128]{2,1,0:T(8,128)(2,1)S(1)}, u32[]{:S(2)}, u32[]{:S(2)}) collective-permute-start(bf16[177,8,128]{2,1,0:T(8,128)(2,1)S(1)} %shard_map.100), channel_id=1, source_target_pairs={{0,6},{2,0},{4,2},{6,4},{1,7},{3,1},{5,3},{7,5},{8,14},{10,8},{12,... | collective-permute-start | bytes 1087496 | tf_op jit(solution)/shard_map/ppermute | solution.py:493
  70.8 0.2 collective-permute-start.10
  71.0 0.7 shard_map.108
  71.7 0.7 collective-permute-start.9
  72.4 0.0 collective-permute-done.12.rb_ref
  72.4 2.5 %collective-permute-start.13 = (bf16[128,1152]{1,0:T(8,128)(2,1)S(1)}, bf16[128,1152]{1,0:T(8,128)(2,1)S(1)}, u32[]{:S(2)}, u32[]{:S(2)}) collective-permute-start(bf16[128,1152]{1,0:T(8,128)(2,1)S(1)} %shard_map.105), channel_id=1, source_target_pairs={{0,6},{2,0},{4,2},{6,4},{1,7},{3,1},{5,3},{7,5},{8,14},{10,8},{12,... | collective-permute-start | bytes 884744 | tf_op jit(solution)/shard_map/ppermute | solution.py:503
  74.9 4.6 %collective-permute-done.11.la_ref = bf16[177,8,128]{2,1,0:T(8,128)(2,1)S(1)} collective-permute-done((bf16[177,8,128]{2,1,0:T(8,128)(2,1)S(1)}, bf16[177,8,128]{2,1,0:T(8,128)(2,1)S(1)}, u32[]{:S(2)}, u32[]{:S(2)}) %collective-permute-start.11) | collective-permute-done | bytes 362528 | tf_op jit(solution)/shard_map/ppermute | solution.py:493
  79.5 6.3 %collective-permute-done.13.lb_ref = bf16[128,1152]{1,0:T(8,128)(2,1)S(1)} collective-permute-done((bf16[128,1152]{1,0:T(8,128)(2,1)S(1)}, bf16[128,1152]{1,0:T(8,128)(2,1)S(1)}, u32[]{:S(2)}, u32[]{:S(2)}) %collective-permute-start.13) | collective-permute-done | bytes 294944 | tf_op jit(solution)/shard_map/ppermute | solution.py:503
  85.8 1.2 %shard_map.109 = bf16[128,2560]{1,0:T(8,128)(2,1)} custom-call(f32[8,128]{1,0:T(8,128)S(1)} %get-tuple-element.94.square_ref, f32[128,1408]{1,0:T(8,128)S(1)} %get-tuple-element.96.ka_ref, f32[128,1152]{1,0:T(8,128)S(1)} %get-tuple-element.99.kb_ref, bf16[136,1408]{1,0:T(8,128)(2,1)S(1)} %collective-permute-done.8.ga_ref, ...), custom_call_target="tpu_custom_call" | custom-call | flops 100000000 | tf_op jit(solution)/shard_map/pallas_call | solution.py:356
  (17 shorter events, 0.0 us)
Async XLA Ops:
  0.0 30.6 %copy-start.3 = (bf16[640]{0:T(1024)(128)(2,1)S(1)}, bf16[640]{0:T(1024)(128)(2,1)}, u32[]{:S(2)}) copy-start(bf16[640]{0:T(1024)(128)(2,1)} %param.16) | copy-start | bytes 3844
  0.0 30.6 %copy-start.4 = (f32[10]{0:T(128)S(1)}, f32[10]{0:T(128)}, u32[]{:S(2)}) copy-start(f32[10]{0:T(128)} %param.15) | copy-start | bytes 124
  26.0 14.2 %all-to-all-start.1 = ((bf16[32,4,640]{2,1,0:T(4,128)(2,1)}), bf16[32,4,640]{2,1,0:T(4,128)(2,1)S(1)}, u32[]{:S(2)}, u32[]{:S(2)}) async-start(bf16[32,4,640]{2,1,0:T(4,128)(2,1)} %shard_map.92), calls=%async_computation.1 | async-start | bytes 327680 | tf_op jit(solution)/shard_map/all_to_all | solution.py:474
  30.9 9.3 %copy-start = (bf16[1024,128]{1,0:T(8,128)(2,1)S(1)}, bf16[1024,128]{1,0:T(8,128)(2,1)}, u32[]{:S(2)}) copy-start(bf16[1024,128]{1,0:T(8,128)(2,1)} %c_ref.7) | copy-start | bytes 786436
  42.0 6.6 %collective-permute-start = (bf16[136,1408]{1,0:T(8,128)(2,1)S(1)}, bf16[136,1408]{1,0:T(8,128)(2,1)S(1)}, u32[]{:S(2)}, u32[]{:S(2)}) collective-permute-start(bf16[136,1408]{1,0:T(8,128)(2,1)S(1)} %get-tuple-element.61), channel_id=1, source_target_pairs={{0,1},{1,0},{2,3},{3,2},{4,5},{5,4},{6,7},{7,6},{8,9},{9,8},{10,11... | collective-permute-start | bytes 1148936 | tf_op jit(solution)/shard_map/ppermute | solution.py:479
  48.4 1.7 %collective-permute-start.1 = (bf16[128,1152]{1,0:T(8,128)(2,1)S(1)}, bf16[128,1152]{1,0:T(8,128)(2,1)S(1)}, u32[]{:S(2)}, u32[]{:S(2)}) collective-permute-start(bf16[128,1152]{1,0:T(8,128)(2,1)S(1)} %get-tuple-element.69), channel_id=1, source_target_pairs={{0,1},{1,0},{2,3},{3,2},{4,5},{5,4},{6,7},{7,6},{8,9},{9,8},{10,11... | collective-permute-start | bytes 884744 | tf_op jit(solution)/shard_map/ppermute | solution.py:483
  50.9 1.8 %collective-permute-start.2 = (bf16[136,1408]{1,0:T(8,128)(2,1)S(1)}, bf16[136,1408]{1,0:T(8,128)(2,1)S(1)}, u32[]{:S(2)}, u32[]{:S(2)}) collective-permute-start(bf16[136,1408]{1,0:T(8,128)(2,1)S(1)} %get-tuple-element.74), channel_id=1, source_target_pairs={{0,1},{1,0},{2,3},{3,2},{4,5},{5,4},{6,7},{7,6},{8,9},{9,8},{10,11... | collective-permute-start | bytes 1148936 | tf_op jit(solution)/shard_map/ppermute | solution.py:489
  51.8 1.7 %collective-permute-start.3 = (bf16[128,1152]{1,0:T(8,128)(2,1)S(1)}, bf16[128,1152]{1,0:T(8,128)(2,1)S(1)}, u32[]{:S(2)}, u32[]{:S(2)}) collective-permute-start(bf16[128,1152]{1,0:T(8,128)(2,1)S(1)} %get-tuple-element.80), channel_id=1, source_target_pairs={{0,1},{1,0},{2,3},{3,2},{4,5},{5,4},{6,7},{7,6},{8,9},{9,8},{10,11... | collective-permute-start | bytes 884744 | tf_op jit(solution)/shard_map/ppermute | solution.py:491
  54.3 11.6 %collective-permute-start.4 = (bf16[136,1408]{1,0:T(8,128)(2,1)S(1)}, bf16[136,1408]{1,0:T(8,128)(2,1)S(1)}, u32[]{:S(2)}, u32[]{:S(2)}) collective-permute-start(bf16[136,1408]{1,0:T(8,128)(2,1)S(1)} %get-tuple-element.84), channel_id=1, source_target_pairs={{0,1},{1,0},{2,3},{3,2},{4,5},{5,4},{6,7},{7,6},{8,9},{9,8},{10,11... | collective-permute-start | bytes 1148936 | tf_op jit(solution)/shard_map/ppermute | solution.py:497
  54.8 11.1 %collective-permute-start.5 = (bf16[177,8,128]{2,1,0:T(8,128)(2,1)S(1)}, bf16[177,8,128]{2,1,0:T(8,128)(2,1)S(1)}, u32[]{:S(2)}, u32[]{:S(2)}) collective-permute-start(bf16[177,8,128]{2,1,0:T(8,128)(2,1)S(1)} %shard_map.96), channel_id=1, source_target_pairs={{0,2},{2,4},{4,6},{6,0},{1,3},{3,5},{5,7},{7,1},{8,10},{10,12},{12... | collective-permute-start | bytes 1087496 | tf_op jit(solution)/shard_map/ppermute | solution.py:486
  56.0 10.0 %collective-permute-start.7 = (bf16[128,1152]{1,0:T(8,128)(2,1)S(1)}, bf16[128,1152]{1,0:T(8,128)(2,1)S(1)}, u32[]{:S(2)}, u32[]{:S(2)}) collective-permute-start(bf16[128,1152]{1,0:T(8,128)(2,1)S(1)} %shard_map.97), channel_id=1, source_target_pairs={{0,6},{2,0},{4,2},{6,4},{1,7},{3,1},{5,3},{7,5},{8,14},{10,8},{12,... | collective-permute-start | bytes 884744 | tf_op jit(solution)/shard_map/ppermute | solution.py:486
  58.1 7.9 %collective-permute-start.6 = (bf16[128,1152]{1,0:T(8,128)(2,1)S(1)}, bf16[128,1152]{1,0:T(8,128)(2,1)S(1)}, u32[]{:S(2)}, u32[]{:S(2)}) collective-permute-start(bf16[128,1152]{1,0:T(8,128)(2,1)S(1)} %get-tuple-element.88), channel_id=1, source_target_pairs={{0,1},{1,0},{2,3},{3,2},{4,5},{5,4},{6,7},{7,6},{8,9},{9,8},{10,11... | collective-permute-start | bytes 884744 | tf_op jit(solution)/shard_map/ppermute | solution.py:499
  58.9 13.5 %collective-permute-start.12 = (bf16[128,1152]{1,0:T(8,128)(2,1)S(1)}, bf16[128,1152]{1,0:T(8,128)(2,1)S(1)}, u32[]{:S(2)}, u32[]{:S(2)}) collective-permute-start(bf16[128,1152]{1,0:T(8,128)(2,1)S(1)} %shard_map.101), channel_id=1, source_target_pairs={{0,2},{2,4},{4,6},{6,0},{1,3},{3,5},{5,7},{7,1},{8,10},{10,12},{12... | collective-permute-start | bytes 884744 | tf_op jit(solution)/shard_map/ppermute | solution.py:495
  58.9 7.2 %copy-start.1 = (bf16[256,640]{1,0:T(8,128)(2,1)S(1)}, bf16[256,640]{1,0:T(8,128)(2,1)}, u32[]{:S(2)}) copy-start(bf16[256,640]{1,0:T(8,128)(2,1)} %get-tuple-element.92.gl_ref) | copy-start | bytes 983044
  58.9 7.2 %copy-start.2 = (bf16[256,640]{1,0:T(8,128)(2,1)S(1)}, bf16[256,640]{1,0:T(8,128)(2,1)}, u32[]{:S(2)}) copy-start(bf16[256,640]{1,0:T(8,128)(2,1)} %get-tuple-element.93.fs_ref) | copy-start | bytes 983044
  67.9 17.9 %collective-permute-start.8 = (bf16[136,1408]{1,0:T(8,128)(2,1)S(1)}, bf16[136,1408]{1,0:T(8,128)(2,1)S(1)}, u32[]{:S(2)}, u32[]{:S(2)}) collective-permute-start(bf16[136,1408]{1,0:T(8,128)(2,1)S(1)} %get-tuple-element.97), channel_id=1, source_target_pairs={{0,1},{1,0},{2,3},{3,2},{4,5},{5,4},{6,7},{7,6},{8,9},{9,8},{10,11... | collective-permute-start | bytes 1148936 | tf_op jit(solution)/shard_map/ppermute | solution.py:507
  69.6 9.9 %collective-permute-start.11 = (bf16[177,8,128]{2,1,0:T(8,128)(2,1)S(1)}, bf16[177,8,128]{2,1,0:T(8,128)(2,1)S(1)}, u32[]{:S(2)}, u32[]{:S(2)}) collective-permute-start(bf16[177,8,128]{2,1,0:T(8,128)(2,1)S(1)} %shard_map.100), channel_id=1, source_target_pairs={{0,6},{2,0},{4,2},{6,4},{1,7},{3,1},{5,3},{7,5},{8,14},{10,8},{12,... | collective-permute-start | bytes 1087496 | tf_op jit(solution)/shard_map/ppermute | solution.py:493
  70.8 15.0 %collective-permute-start.10 = (bf16[177,8,128]{2,1,0:T(8,128)(2,1)S(1)}, bf16[177,8,128]{2,1,0:T(8,128)(2,1)S(1)}, u32[]{:S(2)}, u32[]{:S(2)}) collective-permute-start(bf16[177,8,128]{2,1,0:T(8,128)(2,1)S(1)} %shard_map.104), channel_id=1, source_target_pairs={{0,2},{2,4},{4,6},{6,0},{1,3},{3,5},{5,7},{7,1},{8,10},{10,12},{12... | collective-permute-start | bytes 1087496 | tf_op jit(solution)/shard_map/ppermute | solution.py:501
  71.7 7.8 %collective-permute-start.9 = (bf16[128,1152]{1,0:T(8,128)(2,1)S(1)}, bf16[128,1152]{1,0:T(8,128)(2,1)S(1)}, u32[]{:S(2)}, u32[]{:S(2)}) collective-permute-start(bf16[128,1152]{1,0:T(8,128)(2,1)S(1)} %get-tuple-element.100), channel_id=1, source_target_pairs={{0,1},{1,0},{2,3},{3,2},{4,5},{5,4},{6,7},{7,6},{8,9},{9,8},{10,11... | collective-permute-start | bytes 884744 | tf_op jit(solution)/shard_map/ppermute | solution.py:509
  72.4 13.4 %collective-permute-start.13 = (bf16[128,1152]{1,0:T(8,128)(2,1)S(1)}, bf16[128,1152]{1,0:T(8,128)(2,1)S(1)}, u32[]{:S(2)}, u32[]{:S(2)}) collective-permute-start(bf16[128,1152]{1,0:T(8,128)(2,1)S(1)} %shard_map.105), channel_id=1, source_target_pairs={{0,6},{2,0},{4,2},{6,4},{1,7},{3,1},{5,3},{7,5},{8,14},{10,8},{12,... | collective-permute-start | bytes 884744 | tf_op jit(solution)/shard_map/ppermute | solution.py:503

commit v2 on v1

--- a/solution.py
+++ b/solution.py
@@ -58,14 +58,15 @@
     return jnp.where(row <= lax.broadcasted_iota(jnp.int32, (BLOCK, BLOCK), 1), 1.0, 0.0).astype(BF16)
 
 
-def running_sums(value):
+def running_sums(value, upper):
     rows = value.shape[0]
-    sums = jnp.dot(jnp.concatenate(parts(value, 3), axis=0), triangle(), preferred_element_type=F32)
+    sums = jnp.dot(jnp.concatenate(parts(value, 3), axis=0), upper, preferred_element_type=F32)
     return sums[0:rows] + sums[rows : 2 * rows] + sums[2 * rows : 3 * rows]
 
 
 def state_kernel(
-    x_hbm, b_hbm, dt_hbm, ld_hbm, msg_ref, pad_ref, dtp_ref, run_ref, x_ref, b_ref, dt_ref, ld_ref, sem
+    x_hbm, b_hbm, dt_hbm, ld_hbm, msg_ref, pad_ref, dtp_ref, run_ref, x_ref, b_ref, dt_ref, ld_ref,
+    upper_ref, two_ref, sem
 ):
     copies = [pltpu.make_async_copy(ld_hbm, ld_ref, sem.at[0]), pltpu.make_async_copy(dt_hbm, dt_ref, sem.at[1])]
     for k in range(NBLK):
@@ -76,10 +77,12 @@
         copy.start()
     pad_ref[...] = jnp.zeros_like(pad_ref)
     dtp_ref[...] = jnp.zeros_like(dtp_ref)
+    upper_ref[...] = triangle()
+    two_ref[...] = spread_matrix(2, False)
     copies[0].wait()
     for k in range(NBLK):
         pad_ref[PADH * k : PADH * k + HEADS, :] = ld_ref[:, BLOCK * k : BLOCK * (k + 1)]
-    levels = running_sums(pad_ref[...])
+    levels = running_sums(pad_ref[...], upper_ref[...])
     closings = [levels[PADH * k : PADH * (k + 1), BLOCK - 1 : BLOCK] for k in range(NBLK)]
     tails = [jnp.zeros((PADH, 1), F32)]
     for k in reversed(range(NBLK)):
@@ -88,16 +91,18 @@
     decay = spread(jnp.where(lane == 0, tails[0], 0.0), spread_matrix(3, True)[:, CH:], 3)[0:1, :]
     decays = jnp.concatenate([v.astype(F32) for v in parts(decay, 3)] + [jnp.zeros((1, HALF), F32)], axis=0)
     decays = decays.astype(BF16)
-    two = spread_matrix(2, False)
+    two = two_ref[...]
     copies[1].wait()
     dtp_ref[0:HEADS, :] = dt_ref[...]
+    wides = []
+    for k in range(NBLK):
+        weight = jnp.exp(tails[k] - levels[PADH * k : PADH * (k + 1)]) * dtp_ref[:, BLOCK * k : BLOCK * (k + 1)]
+        wides.append(spread(weight, two, 2))
+    for copy in copies[2:]:
+        copy.wait()
     total = None
     for k in range(NBLK):
-        weight = jnp.exp(tails[k] - levels[PADH * k : PADH * (k + 1)]) * dtp_ref[:, BLOCK * k : BLOCK * (k + 1)]
-        wide = spread(weight, two, 2)
-        copies[2 + 2 * k].wait()
-        copies[3 + 2 * k].wait()
-        weighted = (wide * x_ref[BLOCK * k : BLOCK * (k + 1), :].astype(F32)).astype(BF16)
+        weighted = (wides[k] * x_ref[BLOCK * k : BLOCK * (k + 1), :].astype(F32)).astype(BF16)
         own = lax.dot_general(
             b_ref[BLOCK * k : BLOCK * (k + 1), :], weighted, (((0,), (0,)), ((), ())), preferred_element_type=F32
         )
@@ -151,7 +156,7 @@
 
     pad_ref[0:HEADS, :] = ld_ref[...]
     dtp_ref[0:HEADS, :] = dt_ref[...]
-    lev = running_sums(pad_ref[...])
+    lev = running_sums(pad_ref[...], triangle())
     closing = lev[:, BLOCK - 1 : BLOCK]
     reader, writer = c_ref[...], b_ref[...]
     two = spread_matrix(2, False)
@@ -320,22 +325,27 @@
     return jnp.sum(ref[TILES - 1].astype(F32), axis=0, keepdims=True)
 
 
-def finish_kernel(
-    devices, square_ref, ka_ref, kb_ref, ga_ref, gb_ref, ra_ref, la_ref, rb_ref, lb_ref, out_hbm, scale_ref, out_ref, sem
-):
-    total = square_ref[1:2, :] + squares_of(ga_ref, HALF) + last_squares(ra_ref) + last_squares(la_ref)
+def base_kernel(square_ref, ka_ref, kb_ref, ga_ref, gb_ref, la_ref, rb_ref, base_ref, total_ref):
+    total = square_ref[1:2, :] + squares_of(ga_ref, HALF) + last_squares(la_ref)
+    total_ref[...] = jnp.broadcast_to(total, total_ref.shape)
+    for n, row, lanes in tiles_of(WA):
+        span = slice(row, row + 8)
+        base_ref[span, lanes] = ka_ref[span, lanes] + ga_ref[span, lanes].astype(F32) + la_ref[n].astype(F32)
+    base_ref[:, WA:D] = kb_ref[...] + gb_ref[...].astype(F32) + rb_ref[...].astype(F32)
+
+
+def finish_kernel(devices, total_ref, base_ref, ra_ref, lb_ref, out_hbm, scale_ref, out_ref, sem):
+    total = total_ref[0:1, :] + last_squares(ra_ref)
     scale = lax.rsqrt(total / (CH * devices) + 1e-05)
     scale_ref[...] = jnp.transpose(jnp.broadcast_to(scale, (HALF, HALF)))
     copies = []
     group = HALF // CHUNKS
     for n, row, lanes in tiles_of(WA):
         span = slice(row, row + 8)
-        value = ka_ref[span, lanes] + ga_ref[span, lanes].astype(F32) + ra_ref[n].astype(F32) + la_ref[n].astype(F32)
-        out_ref[span, lanes] = (value * scale_ref[span, 0:1]).astype(BF16)
+        out_ref[span, lanes] = ((base_ref[span, lanes] + ra_ref[n].astype(F32)) * scale_ref[span, 0:1]).astype(BF16)
         if lanes.stop == WA and (row + 8) % group == 0:
             span = slice(row + 8 - group, row + 8)
-            value = kb_ref[span, :] + gb_ref[span, :].astype(F32) + rb_ref[span, :].astype(F32)
-            value = value + lb_ref[span, :].astype(F32)
+            value = base_ref[span, WA:D] + lb_ref[span, :].astype(F32)
             out_ref[span, WA:D] = (value * scale_ref[span, 0:1]).astype(BF16)
             span = pl.ds(row + 8 - group, group)
             copies.append(pltpu.make_async_copy(out_ref.at[span, :], out_hbm.at[span, :], sem.at[len(copies)]))
@@ -376,6 +386,8 @@
         ((ROWS, STATE), BF16),
         ((HEADS, ROWS), F32),
         ((HEADS, ROWS), F32),
+        ((BLOCK, BLOCK), BF16),
+        ((2 * PADH, CH), BF16),
         2 + 2 * NBLK,
     ]
     return local_call(state_kernel, (x, b, dt, ld), outs, scratch, 1e9, [HBM] * 4)[0]
@@ -507,7 +519,9 @@
     got_a = lax.ppermute(send, "c", swap)
     send, keep_b = product(after(rows, send), square, w_b)
     got_b = lax.ppermute(send, "c", swap)
-    return finish(2 * chips, square, keep_a, keep_b, got_a, got_b, right_a, left_a, right_b, left_b)
+    outs = (((HALF, D), F32), ((8, HALF), F32))
+    base, total = local_call(base_kernel, (square, keep_a, keep_b, got_a, got_b, left_a, right_b), outs)
+    return finish(2 * chips, total, base, right_a, left_b)
 
 
 def solution(mesh):

time: 87.4 us -> 86.6 us (level)
    pallas_call x19 -> x20, Pallas kernels: 16 us -> 15.4 us  [local_call(): pl.pallas_call(kernel, in_specs=in_specs, out_specs=out_specs, out_shape=...]
  transfers between devices with their start and end apart: 15 -> 15, of which waited for: 7 -> 7; matrix products, arithmetic and copies ran while one was open for 0% -> 0% of each run, Pallas kernels for 18% -> 19%
where the time goes in v2:
time: 86.6 us; the launch traced here: 86.4 us
  Pallas kernels  24.1 us (28%)
  blocking collectives  21.8 us (25%)
  waiting for transfers between devices  20.8 us (24%)
  starting transfers between devices  19 us (22%)
    all_to_all x1, blocking collectives, body(): lax.all_to_all(msg, ('z', 'y'), split_axis=0, concat_axis=0, tiled=True)  21.8 us
    pallas_call x20, Pallas kernels, local_call(): pl.pallas_call(kernel, in_specs=in_specs, out_specs=out_specs, out_shape=...  15.4 us
    pallas_call x1, Pallas kernels, local_part(): pl.pallas_call(local_kernel, grid=(NBLK,), in_specs=[SMEM, rows(CH), rows...  8.66 us
    ppermute x1, waiting for transfers between devices, body(): lax.ppermute(far_a, 'x', up)  6.94 us
    ppermute x1, waiting for transfers between devices, body(): left_b = lax.ppermute(left_b, 'x', down)  6.11 us
    all_to_all x1, starting transfers between devices, body(): lax.all_to_all(seq_prefix(msg), ('z', 'y'), split_axis=0, concat_axis=0,...  4.62 us
    ppermute x1, waiting for transfers between devices, body(): left_a = lax.ppermute(left_a, 'x', down)  4.56 us
    ppermute x1, starting transfers between devices, body(): far_got_a = lax.ppermute(send, 'c', swap)  3.31 us
  transfers between devices with their start and end apart: 15, of which 7 were waited for; matrix products, arithmetic and copies ran while one was open for 0% of the time, Pallas kernels for 19%

profile of v2, /device:TPU:1, one launch (start us, length us, event | category | flops | bytes accessed | tf_op | source)
XLA Modules:
  0.0 86.4 jit_solution(12895462512610091227)
XLA Ops:
  0.0 2.4 %shard_map.91 = bf16[32,4,768]{2,1,0:T(4,128)(2,1)S(1)} custom-call(bf16[1024,640]{1,0:T(8,128)(2,1)} %x_ref.1, bf16[1024,128]{1,0:T(8,128)(2,1)} %b_ref.1, f32[10,1024]{1,0:T(8,128)} %bitcast.7, f32[10,1024]{1,0:T(8,128)} %bitcast.9), custom_call_target="tpu_custom_call" | custom-call | flops 1000000000 | tf_op jit(solution)/shard_map/pallas_call | solution.py:366
  2.4 21.8 %all_to_all.10.msg_ref = bf16[32,4,768]{2,1,0:T(4,128)(2,1)S(1)} all-to-all(bf16[32,4,768]{2,1,0:T(4,128)(2,1)S(1)} %shard_map.91), channel_id=1, replica_groups=mesh['z'=8,'y'=4,'x'=4,'c'=2] {'z','y'}, dimensions={0} | all-to-all | bytes 393216 | tf_op jit(solution)/shard_map/all_to_all | solution.py:482
  24.2 1.0 %shard_map.92 = bf16[32,4,640]{2,1,0:T(4,128)(2,1)} custom-call(bf16[32,4,768]{2,1,0:T(4,128)(2,1)S(1)} %all_to_all.10.msg_ref), custom_call_target="tpu_custom_call" | custom-call | flops 100000000 | tf_op jit(solution)/shard_map/pallas_call | solution.py:366
  25.2 4.6 %all-to-all-start.1 = ((bf16[32,4,640]{2,1,0:T(4,128)(2,1)}), bf16[32,4,640]{2,1,0:T(4,128)(2,1)S(1)}, u32[]{:S(2)}, u32[]{:S(2)}) async-start(bf16[32,4,640]{2,1,0:T(4,128)(2,1)} %shard_map.92), calls=%async_computation.1 | async-start | bytes 327680 | tf_op jit(solution)/shard_map/all_to_all | solution.py:486
  29.9 0.1 broadcast_in_dim.10
  30.0 0.1 broadcast_in_dim_reshape.3.skip_ref
  30.1 0.1 stack.23.idx_ref
  30.2 8.7 %local_part.1 = (bf16[256,640]{1,0:T(8,128)(2,1)S(1)}, bf16[256,640]{1,0:T(8,128)(2,1)S(1)}, bf16[256,640]{1,0:T(8,128)(2,1)S(1)}, bf16[256,640]{1,0:T(8,128)(2,...) custom-call(s32[5]{0:T(128)S(1)} %stack.23.idx_ref, ...), custom_call_target="tpu_custom_call" | custom-call | flops 3000000000 | tf_op jit(solution)/shard_map/local_part/pallas_call | solution.py:410
  38.8 0.6 all-to-all-done.1.p_ref
  39.5 1.0 %shard_map.93 = (bf16[256,640]{1,0:T(8,128)(2,1)S(1)}, f32[8,128]{1,0:T(8,128)S(1)}, bf16[128,640]{1,0:T(8,128)(2,1)S(1)}) custom-call(s32[5]{0:T(128)S(1)} %stack.23.idx_ref, bf16[32,4,640]{2,1,0:T(4,128)(2,1)S(1)} %all-to-all-done.1.p_ref, f32[1,640]{1,0:T(1,128)S(1)} %reshape.gain_ref, bf16[1024,128]{1,0:T(8,128)(2,1)S(1)} %copy-done, ...), custom_call_target="tpu_custom_call" | custom-call | flops 500000000 | tf_op jit(solution)/shard_map/pallas_call | solution.py:366
  40.5 0.8 shard_map.94
  41.3 3.3 %collective-permute-start = (bf16[136,1408]{1,0:T(8,128)(2,1)S(1)}, bf16[136,1408]{1,0:T(8,128)(2,1)S(1)}, u32[]{:S(2)}, u32[]{:S(2)}) collective-permute-start(bf16[136,1408]{1,0:T(8,128)(2,1)S(1)} %get-tuple-element.63), channel_id=1, source_target_pairs={{0,1},{1,0},{2,3},{3,2},{4,5},{5,4},{6,7},{7,6},{8,9},{9,8},{10,11... | collective-permute-start | bytes 1148936 | tf_op jit(solution)/shard_map/ppermute | solution.py:491
  44.6 3.1 %shard_map.95 = (bf16[128,1152]{1,0:T(8,128)(2,1)S(1)}, f32[128,1152]{1,0:T(8,128)S(1)}, bf16[256,640]{1,0:T(8,128)(2,1)S(1)}, f32[8,128]{1,0:T(8,128)S(1)}, bf1...) custom-call(s32[5]{0:T(128)S(1)} %stack.23.idx_ref, ...), custom_call_target="tpu_custom_call" | custom-call | flops 2000000000 | tf_op jit(solution)/shard_map/pallas_call | solution.py:366
  47.7 0.1 collective-permute-start.1
  47.8 0.0 collective-permute-done.got_ref
  47.8 0.1 shard_map.96
  47.9 1.5 %collective-permute-done.1.got_ref = bf16[128,1152]{1,0:T(8,128)(2,1)S(1)} collective-permute-done((bf16[128,1152]{1,0:T(8,128)(2,1)S(1)}, bf16[128,1152]{1,0:T(8,128)(2,1)S(1)}, u32[]{:S(2)}, u32[]{:S(2)}) %collective-permute-start.1) | collective-permute-done | bytes 294944 | tf_op jit(solution)/shard_map/ppermute | solution.py:495
  49.4 0.1 shard_map.97
  49.4 0.8 shard_map.98
  50.2 0.2 collective-permute-start.2
  50.4 0.7 shard_map.99
  51.1 0.5 collective-permute-start.3
  51.6 0.4 collective-permute-done.2.got_ref
  52.0 0.1 shard_map.100
  52.1 0.7 collective-permute-done.3.got_ref
  52.8 0.1 shard_map.101
  52.8 0.8 shard_map.102
  53.6 0.5 collective-permute-start.4
  54.1 1.2 %collective-permute-start.5 = (bf16[177,8,128]{2,1,0:T(8,128)(2,1)S(1)}, bf16[177,8,128]{2,1,0:T(8,128)(2,1)S(1)}, u32[]{:S(2)}, u32[]{:S(2)}) collective-permute-start(bf16[177,8,128]{2,1,0:T(8,128)(2,1)S(1)} %shard_map.96), channel_id=1, source_target_pairs={{0,2},{2,4},{4,6},{6,0},{1,3},{3,5},{5,7},{7,1},{8,10},{10,12},{12... | collective-permute-start | bytes 1087496 | tf_op jit(solution)/shard_map/ppermute | solution.py:498
  55.3 1.5 %collective-permute-start.7 = (bf16[128,1152]{1,0:T(8,128)(2,1)S(1)}, bf16[128,1152]{1,0:T(8,128)(2,1)S(1)}, u32[]{:S(2)}, u32[]{:S(2)}) collective-permute-start(bf16[128,1152]{1,0:T(8,128)(2,1)S(1)} %shard_map.97), channel_id=1, source_target_pairs={{0,6},{2,0},{4,2},{6,4},{1,7},{3,1},{5,3},{7,5},{8,14},{10,8},{12,... | collective-permute-start | bytes 884744 | tf_op jit(solution)/shard_map/ppermute | solution.py:498
  56.7 0.7 shard_map.103
  57.4 0.8 collective-permute-start.6
  58.2 0.0 collective-permute-start.11
  58.2 6.9 %collective-permute-done.5.refs_1_ = bf16[177,8,128]{2,1,0:T(8,128)(2,1)S(1)} collective-permute-done((bf16[177,8,128]{2,1,0:T(8,128)(2,1)S(1)}, bf16[177,8,128]{2,1,0:T(8,128)(2,1)S(1)}, u32[]{:S(2)}, u32[]{:S(2)}) %collective-permute-start.5) | collective-permute-done | bytes 362528 | tf_op jit(solution)/shard_map/ppermute | solution.py:498
  65.1 0.1 shard_map.104
  65.3 0.1 shard_map.105
  65.4 1.0 %shard_map.106 = (bf16[256,640]{1,0:T(8,128)(2,1)S(1)}, f32[8,128]{1,0:T(8,128)S(1)}) custom-call(s32[5]{0:T(128)S(1)} %stack.23.idx_ref, bf16[128,640]{1,0:T(8,128)(2,1)S(1)} %get-tuple-element.93.p_ref, f32[1,640]{1,0:T(1,128)S(1)} %reshape.gain_ref, bf16[1024,128]{1,0:T(8,128)(2,1)S(1)} %copy-done, bf16[256,640]{1,0:T(8,128)(2,1)S(1)} %copy-done.1, ...), custom_call_target="tpu_custom_call" | custom-call | flops 500000000 | tf_op jit(solution)/shard_map/pallas_call | solution.py:366
  66.4 0.8 shard_map.107
  67.2 1.7 %collective-permute-start.8 = (bf16[136,1408]{1,0:T(8,128)(2,1)S(1)}, bf16[136,1408]{1,0:T(8,128)(2,1)S(1)}, u32[]{:S(2)}, u32[]{:S(2)}) collective-permute-start(bf16[136,1408]{1,0:T(8,128)(2,1)S(1)} %get-tuple-element.99), channel_id=1, source_target_pairs={{0,1},{1,0},{2,3},{3,2},{4,5},{5,4},{6,7},{7,6},{8,9},{9,8},{10,11... | collective-permute-start | bytes 1148936 | tf_op jit(solution)/shard_map/ppermute | solution.py:519
  68.8 1.3 %collective-permute-start.10 = (bf16[177,8,128]{2,1,0:T(8,128)(2,1)S(1)}, bf16[177,8,128]{2,1,0:T(8,128)(2,1)S(1)}, u32[]{:S(2)}, u32[]{:S(2)}) collective-permute-start(bf16[177,8,128]{2,1,0:T(8,128)(2,1)S(1)} %shard_map.100), channel_id=1, source_target_pairs={{0,6},{2,0},{4,2},{6,4},{1,7},{3,1},{5,3},{7,5},{8,14},{10,8},{12,... | collective-permute-start | bytes 1087496 | tf_op jit(solution)/shard_map/ppermute | solution.py:505
  70.1 0.2 collective-permute-start.12
  70.3 0.7 shard_map.108
  71.0 0.7 collective-permute-start.9
  71.7 2.5 %collective-permute-start.13 = (bf16[128,1152]{1,0:T(8,128)(2,1)S(1)}, bf16[128,1152]{1,0:T(8,128)(2,1)S(1)}, u32[]{:S(2)}, u32[]{:S(2)}) collective-permute-start(bf16[128,1152]{1,0:T(8,128)(2,1)S(1)} %shard_map.105), channel_id=1, source_target_pairs={{0,6},{2,0},{4,2},{6,4},{1,7},{3,1},{5,3},{7,5},{8,14},{10,8},{12,... | collective-permute-start | bytes 884744 | tf_op jit(solution)/shard_map/ppermute | solution.py:515
  74.2 4.6 %collective-permute-done.10.la_ref = bf16[177,8,128]{2,1,0:T(8,128)(2,1)S(1)} collective-permute-done((bf16[177,8,128]{2,1,0:T(8,128)(2,1)S(1)}, bf16[177,8,128]{2,1,0:T(8,128)(2,1)S(1)}, u32[]{:S(2)}, u32[]{:S(2)}) %collective-permute-start.10) | collective-permute-done | bytes 362528 | tf_op jit(solution)/shard_map/ppermute | solution.py:505
  78.8 0.2 shard_map.109
  79.0 6.1 %collective-permute-done.13.lb_ref = bf16[128,1152]{1,0:T(8,128)(2,1)S(1)} collective-permute-done((bf16[128,1152]{1,0:T(8,128)(2,1)S(1)}, bf16[128,1152]{1,0:T(8,128)(2,1)S(1)}, u32[]{:S(2)}, u32[]{:S(2)}) %collective-permute-start.13) | collective-permute-done | bytes 294944 | tf_op jit(solution)/shard_map/ppermute | solution.py:515
  85.1 1.1 %shard_map.110 = bf16[128,2560]{1,0:T(8,128)(2,1)} custom-call(f32[8,128]{1,0:T(8,128)S(1)} %get-tuple-element.103.total_ref, f32[128,2560]{1,0:T(8,128)S(1)} %get-tuple-element.104.base_ref, bf16[177,8,128]{2,1,0:T(8,128)(2,1)S(1)} %collective-permute-done.12.ra_ref, bf16[128,1152]{1,0:T(8,128)(2,1)S(1)} %collective-permute-done.13.lb_ref), custom_call_target="tpu_custom_call" | custom-call | flops 100000000 | tf_op jit(solution)/shard_map/pallas_call | solution.py:366
  (18 shorter events, 0.0 us)
Async XLA Ops:
  0.0 29.9 %copy-start.3 = (bf16[640]{0:T(1024)(128)(2,1)S(1)}, bf16[640]{0:T(1024)(128)(2,1)}, u32[]{:S(2)}) copy-start(bf16[640]{0:T(1024)(128)(2,1)} %param.16) | copy-start | bytes 3844
  0.0 29.9 %copy-start.4 = (f32[10]{0:T(128)S(1)}, f32[10]{0:T(128)}, u32[]{:S(2)}) copy-start(f32[10]{0:T(128)} %param.15) | copy-start | bytes 124
  25.2 14.2 %all-to-all-start.1 = ((bf16[32,4,640]{2,1,0:T(4,128)(2,1)}), bf16[32,4,640]{2,1,0:T(4,128)(2,1)S(1)}, u32[]{:S(2)}, u32[]{:S(2)}) async-start(bf16[32,4,640]{2,1,0:T(4,128)(2,1)} %shard_map.92), calls=%async_computation.1 | async-start | bytes 327680 | tf_op jit(solution)/shard_map/all_to_all | solution.py:486
  30.2 9.3 %copy-start = (bf16[1024,128]{1,0:T(8,128)(2,1)S(1)}, bf16[1024,128]{1,0:T(8,128)(2,1)}, u32[]{:S(2)}) copy-start(bf16[1024,128]{1,0:T(8,128)(2,1)} %c_ref.7) | copy-start | bytes 786436
  41.3 6.6 %collective-permute-start = (bf16[136,1408]{1,0:T(8,128)(2,1)S(1)}, bf16[136,1408]{1,0:T(8,128)(2,1)S(1)}, u32[]{:S(2)}, u32[]{:S(2)}) collective-permute-start(bf16[136,1408]{1,0:T(8,128)(2,1)S(1)} %get-tuple-element.63), channel_id=1, source_target_pairs={{0,1},{1,0},{2,3},{3,2},{4,5},{5,4},{6,7},{7,6},{8,9},{9,8},{10,11... | collective-permute-start | bytes 1148936 | tf_op jit(solution)/shard_map/ppermute | solution.py:491
  47.7 1.7 %collective-permute-start.1 = (bf16[128,1152]{1,0:T(8,128)(2,1)S(1)}, bf16[128,1152]{1,0:T(8,128)(2,1)S(1)}, u32[]{:S(2)}, u32[]{:S(2)}) collective-permute-start(bf16[128,1152]{1,0:T(8,128)(2,1)S(1)} %get-tuple-element.71), channel_id=1, source_target_pairs={{0,1},{1,0},{2,3},{3,2},{4,5},{5,4},{6,7},{7,6},{8,9},{9,8},{10,11... | collective-permute-start | bytes 884744 | tf_op jit(solution)/shard_map/ppermute | solution.py:495
  50.2 1.8 %collective-permute-start.2 = (bf16[136,1408]{1,0:T(8,128)(2,1)S(1)}, bf16[136,1408]{1,0:T(8,128)(2,1)S(1)}, u32[]{:S(2)}, u32[]{:S(2)}) collective-permute-start(bf16[136,1408]{1,0:T(8,128)(2,1)S(1)} %get-tuple-element.76), channel_id=1, source_target_pairs={{0,1},{1,0},{2,3},{3,2},{4,5},{5,4},{6,7},{7,6},{8,9},{9,8},{10,11... | collective-permute-start | bytes 1148936 | tf_op jit(solution)/shard_map/ppermute | solution.py:501
  51.1 1.7 %collective-permute-start.3 = (bf16[128,1152]{1,0:T(8,128)(2,1)S(1)}, bf16[128,1152]{1,0:T(8,128)(2,1)S(1)}, u32[]{:S(2)}, u32[]{:S(2)}) collective-permute-start(bf16[128,1152]{1,0:T(8,128)(2,1)S(1)} %get-tuple-element.82), channel_id=1, source_target_pairs={{0,1},{1,0},{2,3},{3,2},{4,5},{5,4},{6,7},{7,6},{8,9},{9,8},{10,11... | collective-permute-start | bytes 884744 | tf_op jit(solution)/shard_map/ppermute | solution.py:503
  53.6 11.5 %collective-permute-start.4 = (bf16[136,1408]{1,0:T(8,128)(2,1)S(1)}, bf16[136,1408]{1,0:T(8,128)(2,1)S(1)}, u32[]{:S(2)}, u32[]{:S(2)}) collective-permute-start(bf16[136,1408]{1,0:T(8,128)(2,1)S(1)} %get-tuple-element.86), channel_id=1, source_target_pairs={{0,1},{1,0},{2,3},{3,2},{4,5},{5,4},{6,7},{7,6},{8,9},{9,8},{10,11... | collective-permute-start | bytes 1148936 | tf_op jit(solution)/shard_map/ppermute | solution.py:509
  54.1 11.1 %collective-permute-start.5 = (bf16[177,8,128]{2,1,0:T(8,128)(2,1)S(1)}, bf16[177,8,128]{2,1,0:T(8,128)(2,1)S(1)}, u32[]{:S(2)}, u32[]{:S(2)}) collective-permute-start(bf16[177,8,128]{2,1,0:T(8,128)(2,1)S(1)} %shard_map.96), channel_id=1, source_target_pairs={{0,2},{2,4},{4,6},{6,0},{1,3},{3,5},{5,7},{7,1},{8,10},{10,12},{12... | collective-permute-start | bytes 1087496 | tf_op jit(solution)/shard_map/ppermute | solution.py:498
  55.3 10.0 %collective-permute-start.7 = (bf16[128,1152]{1,0:T(8,128)(2,1)S(1)}, bf16[128,1152]{1,0:T(8,128)(2,1)S(1)}, u32[]{:S(2)}, u32[]{:S(2)}) collective-permute-start(bf16[128,1152]{1,0:T(8,128)(2,1)S(1)} %shard_map.97), channel_id=1, source_target_pairs={{0,6},{2,0},{4,2},{6,4},{1,7},{3,1},{5,3},{7,5},{8,14},{10,8},{12,... | collective-permute-start | bytes 884744 | tf_op jit(solution)/shard_map/ppermute | solution.py:498
  57.4 7.9 %collective-permute-start.6 = (bf16[128,1152]{1,0:T(8,128)(2,1)S(1)}, bf16[128,1152]{1,0:T(8,128)(2,1)S(1)}, u32[]{:S(2)}, u32[]{:S(2)}) collective-permute-start(bf16[128,1152]{1,0:T(8,128)(2,1)S(1)} %get-tuple-element.90), channel_id=1, source_target_pairs={{0,1},{1,0},{2,3},{3,2},{4,5},{5,4},{6,7},{7,6},{8,9},{9,8},{10,11... | collective-permute-start | bytes 884744 | tf_op jit(solution)/shard_map/ppermute | solution.py:511
  58.2 13.5 %collective-permute-start.11 = (bf16[128,1152]{1,0:T(8,128)(2,1)S(1)}, bf16[128,1152]{1,0:T(8,128)(2,1)S(1)}, u32[]{:S(2)}, u32[]{:S(2)}) collective-permute-start(bf16[128,1152]{1,0:T(8,128)(2,1)S(1)} %shard_map.101), channel_id=1, source_target_pairs={{0,2},{2,4},{4,6},{6,0},{1,3},{3,5},{5,7},{7,1},{8,10},{10,12},{12... | collective-permute-start | bytes 884744 | tf_op jit(solution)/shard_map/ppermute | solution.py:507
  58.2 7.2 %copy-start.1 = (bf16[256,640]{1,0:T(8,128)(2,1)S(1)}, bf16[256,640]{1,0:T(8,128)(2,1)}, u32[]{:S(2)}) copy-start(bf16[256,640]{1,0:T(8,128)(2,1)} %get-tuple-element.94.gl_ref) | copy-start | bytes 983044
  58.2 7.2 %copy-start.2 = (bf16[256,640]{1,0:T(8,128)(2,1)S(1)}, bf16[256,640]{1,0:T(8,128)(2,1)}, u32[]{:S(2)}) copy-start(bf16[256,640]{1,0:T(8,128)(2,1)} %get-tuple-element.95.fs_ref) | copy-start | bytes 983044
  67.2 11.6 %collective-permute-start.8 = (bf16[136,1408]{1,0:T(8,128)(2,1)S(1)}, bf16[136,1408]{1,0:T(8,128)(2,1)S(1)}, u32[]{:S(2)}, u32[]{:S(2)}) collective-permute-start(bf16[136,1408]{1,0:T(8,128)(2,1)S(1)} %get-tuple-element.99), channel_id=1, source_target_pairs={{0,1},{1,0},{2,3},{3,2},{4,5},{5,4},{6,7},{7,6},{8,9},{9,8},{10,11... | collective-permute-start | bytes 1148936 | tf_op jit(solution)/shard_map/ppermute | solution.py:519
  68.8 9.9 %collective-permute-start.10 = (bf16[177,8,128]{2,1,0:T(8,128)(2,1)S(1)}, bf16[177,8,128]{2,1,0:T(8,128)(2,1)S(1)}, u32[]{:S(2)}, u32[]{:S(2)}) collective-permute-start(bf16[177,8,128]{2,1,0:T(8,128)(2,1)S(1)} %shard_map.100), channel_id=1, source_target_pairs={{0,6},{2,0},{4,2},{6,4},{1,7},{3,1},{5,3},{7,5},{8,14},{10,8},{12,... | collective-permute-start | bytes 1087496 | tf_op jit(solution)/shard_map/ppermute | solution.py:505
  70.1 15.0 %collective-permute-start.12 = (bf16[177,8,128]{2,1,0:T(8,128)(2,1)S(1)}, bf16[177,8,128]{2,1,0:T(8,128)(2,1)S(1)}, u32[]{:S(2)}, u32[]{:S(2)}) collective-permute-start(bf16[177,8,128]{2,1,0:T(8,128)(2,1)S(1)} %shard_map.104), channel_id=1, source_target_pairs={{0,2},{2,4},{4,6},{6,0},{1,3},{3,5},{5,7},{7,1},{8,10},{10,12},{12... | collective-permute-start | bytes 1087496 | tf_op jit(solution)/shard_map/ppermute | solution.py:513
  71.0 7.8 %collective-permute-start.9 = (bf16[128,1152]{1,0:T(8,128)(2,1)S(1)}, bf16[128,1152]{1,0:T(8,128)(2,1)S(1)}, u32[]{:S(2)}, u32[]{:S(2)}) collective-permute-start(bf16[128,1152]{1,0:T(8,128)(2,1)S(1)} %get-tuple-element.102), channel_id=1, source_target_pairs={{0,1},{1,0},{2,3},{3,2},{4,5},{5,4},{6,7},{7,6},{8,9},{9,8},{10,11... | collective-permute-start | bytes 884744 | tf_op jit(solution)/shard_map/ppermute | solution.py:521
  71.7 13.4 %collective-permute-start.13 = (bf16[128,1152]{1,0:T(8,128)(2,1)S(1)}, bf16[128,1152]{1,0:T(8,128)(2,1)S(1)}, u32[]{:S(2)}, u32[]{:S(2)}) collective-permute-start(bf16[128,1152]{1,0:T(8,128)(2,1)S(1)} %shard_map.105), channel_id=1, source_target_pairs={{0,6},{2,0},{4,2},{6,4},{1,7},{3,1},{5,3},{7,5},{8,14},{10,8},{12,... | collective-permute-start | bytes 884744 | tf_op jit(solution)/shard_map/ppermute | solution.py:515

commit v3 on v2

--- a/solution.py
+++ b/solution.py
@@ -236,17 +236,16 @@
 
 
 def gate_block(place, idx_ref, state, gain, c_ref, gl_ref, fs_ref, rows_ref, square_ref):
-    squares = []
-    for n, half in enumerate((1 - idx_ref[0], idx_ref[0])):
-        there = pl.ds(pl.multiple_of((2 * idx_ref[place] + half) * HALF, HALF), HALF)
-        here = pl.ds(pl.multiple_of(half * HALF, HALF), HALF)
-        gated = gl_ref[here, :].astype(F32) + fs_ref[here, :].astype(F32) * jnp.dot(
-            c_ref[there, :], state, preferred_element_type=F32
-        )
-        sums = jnp.sum(gated * gated, axis=1, keepdims=True)
-        squares.append(jnp.transpose(jnp.broadcast_to(sums, (HALF, HALF)))[0:1, :])
-        rows_ref[HALF * n : HALF * (n + 1), :] = (gated * gain).astype(BF16)
-    square_ref[...] = jnp.concatenate(squares + [jnp.zeros((8 - len(squares), HALF), F32)], axis=0)
+    there = pl.ds(pl.multiple_of(idx_ref[place] * BLOCK, BLOCK), BLOCK)
+    product = jnp.dot(c_ref[there, :], state, preferred_element_type=F32)
+    gated = gl_ref[...].astype(F32) + fs_ref[...].astype(F32) * product
+    sums = jnp.sum(gated * gated, axis=1, keepdims=True)
+    value = (gated * gain).astype(BF16)
+    square_ref[...] = jnp.zeros_like(square_ref)
+    for half, n in enumerate((1 - idx_ref[0], idx_ref[0])):
+        span = slice(HALF * half, HALF * (half + 1))
+        rows_ref[pl.ds(pl.multiple_of(n * HALF, HALF), HALF), :] = value[span]
+        square_ref[pl.ds(n, 1), :] = jnp.transpose(jnp.broadcast_to(sums[span], (HALF, HALF)))[0:1, :]
 
 
 def gate_kernel(place, idx_ref, p_ref, gain_ref, c_ref, gl_ref, fs_ref, rows_ref, square_ref, *rest):

time: 86.6 us -> 86.5 us (level)
  no operation moved by 1% of the time
where the time goes in v3:
time: 86.5 us; the launch traced here: 86.2 us
  Pallas kernels  24 us (28%)
  blocking collectives  21.8 us (25%)
  waiting for transfers between devices  20.9 us (24%)
  starting transfers between devices  19 us (22%)
    all_to_all x1, blocking collectives, body(): lax.all_to_all(msg, ('z', 'y'), split_axis=0, concat_axis=0, tiled=True)  21.8 us
    pallas_call x20, Pallas kernels, local_call(): pl.pallas_call(kernel, in_specs=in_specs, out_specs=out_specs, out_shape=...  15.3 us
    pallas_call x1, Pallas kernels, local_part(): pl.pallas_call(local_kernel, grid=(NBLK,), in_specs=[SMEM, rows(CH), rows...  8.66 us
    ppermute x1, waiting for transfers between devices, body(): lax.ppermute(far_a, 'x', up)  6.93 us
    ppermute x1, waiting for transfers between devices, body(): left_b = lax.ppermute(left_b, 'x', down)  6.11 us
    all_to_all x1, starting transfers between devices, body(): lax.all_to_all(seq_prefix(msg), ('z', 'y'), split_axis=0, concat_axis=0,...  4.62 us
    ppermute x1, waiting for transfers between devices, body(): left_a = lax.ppermute(left_a, 'x', down)  4.58 us
    ppermute x1, starting transfers between devices, body(): far_got_a = lax.ppermute(send, 'c', swap)  3.31 us
  transfers between devices with their start and end apart: 15, of which 7 were waited for; matrix products, arithmetic and copies ran while one was open for 0% of the time, Pallas kernels for 19%

profile of v3, /device:TPU:1, one launch (start us, length us, event | category | flops | bytes accessed | tf_op | source)
XLA Modules:
  0.0 86.2 jit_solution(10694799542705912648)
XLA Ops:
  0.0 2.4 %shard_map.91 = bf16[32,4,768]{2,1,0:T(4,128)(2,1)S(1)} custom-call(bf16[1024,640]{1,0:T(8,128)(2,1)} %x_ref.1, bf16[1024,128]{1,0:T(8,128)(2,1)} %b_ref.1, f32[10,1024]{1,0:T(8,128)} %bitcast.7, f32[10,1024]{1,0:T(8,128)} %bitcast.9), custom_call_target="tpu_custom_call" | custom-call | flops 1000000000 | tf_op jit(solution)/shard_map/pallas_call | solution.py:365
  2.4 21.8 %all_to_all.10.msg_ref = bf16[32,4,768]{2,1,0:T(4,128)(2,1)S(1)} all-to-all(bf16[32,4,768]{2,1,0:T(4,128)(2,1)S(1)} %shard_map.91), channel_id=1, replica_groups=mesh['z'=8,'y'=4,'x'=4,'c'=2] {'z','y'}, dimensions={0} | all-to-all | bytes 393216 | tf_op jit(solution)/shard_map/all_to_all | solution.py:481
  24.2 1.0 %shard_map.92 = bf16[32,4,640]{2,1,0:T(4,128)(2,1)} custom-call(bf16[32,4,768]{2,1,0:T(4,128)(2,1)S(1)} %all_to_all.10.msg_ref), custom_call_target="tpu_custom_call" | custom-call | flops 100000000 | tf_op jit(solution)/shard_map/pallas_call | solution.py:365
  25.2 4.6 %all-to-all-start.1 = ((bf16[32,4,640]{2,1,0:T(4,128)(2,1)}), bf16[32,4,640]{2,1,0:T(4,128)(2,1)S(1)}, u32[]{:S(2)}, u32[]{:S(2)}) async-start(bf16[32,4,640]{2,1,0:T(4,128)(2,1)} %shard_map.92), calls=%async_computation.1 | async-start | bytes 327680 | tf_op jit(solution)/shard_map/all_to_all | solution.py:485
  29.9 0.1 broadcast_in_dim.10
  30.0 0.1 broadcast_in_dim_reshape.3.skip_ref
  30.1 0.1 stack.23.idx_ref
  30.2 8.7 %local_part.1 = (bf16[256,640]{1,0:T(8,128)(2,1)S(1)}, bf16[256,640]{1,0:T(8,128)(2,1)S(1)}, bf16[256,640]{1,0:T(8,128)(2,1)S(1)}, bf16[256,640]{1,0:T(8,128)(2,...) custom-call(s32[5]{0:T(128)S(1)} %stack.23.idx_ref, ...), custom_call_target="tpu_custom_call" | custom-call | flops 3000000000 | tf_op jit(solution)/shard_map/local_part/pallas_call | solution.py:409
  38.8 0.6 all-to-all-done.1.p_ref
  39.5 1.0 %shard_map.93 = (bf16[256,640]{1,0:T(8,128)(2,1)S(1)}, f32[8,128]{1,0:T(8,128)S(1)}, bf16[128,640]{1,0:T(8,128)(2,1)S(1)}) custom-call(s32[5]{0:T(128)S(1)} %stack.23.idx_ref, bf16[32,4,640]{2,1,0:T(4,128)(2,1)S(1)} %all-to-all-done.1.p_ref, f32[1,640]{1,0:T(1,128)S(1)} %reshape.gain_ref, bf16[1024,128]{1,0:T(8,128)(2,1)S(1)} %copy-done, ...), custom_call_target="tpu_custom_call" | custom-call | flops 500000000 | tf_op jit(solution)/shard_map/pallas_call | solution.py:365
  40.5 0.8 shard_map.94
  41.3 3.3 %collective-permute-start = (bf16[136,1408]{1,0:T(8,128)(2,1)S(1)}, bf16[136,1408]{1,0:T(8,128)(2,1)S(1)}, u32[]{:S(2)}, u32[]{:S(2)}) collective-permute-start(bf16[136,1408]{1,0:T(8,128)(2,1)S(1)} %get-tuple-element.63), channel_id=1, source_target_pairs={{0,1},{1,0},{2,3},{3,2},{4,5},{5,4},{6,7},{7,6},{8,9},{9,8},{10,11... | collective-permute-start | bytes 1148936 | tf_op jit(solution)/shard_map/ppermute | solution.py:490
  44.6 3.0 %shard_map.95 = (bf16[128,1152]{1,0:T(8,128)(2,1)S(1)}, f32[128,1152]{1,0:T(8,128)S(1)}, bf16[256,640]{1,0:T(8,128)(2,1)S(1)}, f32[8,128]{1,0:T(8,128)S(1)}, bf1...) custom-call(s32[5]{0:T(128)S(1)} %stack.23.idx_ref, ...), custom_call_target="tpu_custom_call" | custom-call | flops 2000000000 | tf_op jit(solution)/shard_map/pallas_call | solution.py:365
  47.6 0.1 collective-permute-start.1
  47.7 0.0 collective-permute-done.got_ref
  47.7 0.1 shard_map.96
  47.8 1.5 %collective-permute-done.1.got_ref = bf16[128,1152]{1,0:T(8,128)(2,1)S(1)} collective-permute-done((bf16[128,1152]{1,0:T(8,128)(2,1)S(1)}, bf16[128,1152]{1,0:T(8,128)(2,1)S(1)}, u32[]{:S(2)}, u32[]{:S(2)}) %collective-permute-start.1) | collective-permute-done | bytes 294944 | tf_op jit(solution)/shard_map/ppermute | solution.py:494
  49.2 0.1 shard_map.97
  49.3 0.8 shard_map.98
  50.1 0.2 collective-permute-start.2
  50.3 0.7 shard_map.99
  50.9 0.5 collective-permute-start.3
  51.4 0.4 collective-permute-done.2.got_ref
  51.9 0.1 shard_map.100
  52.0 0.6 collective-permute-done.3.got_ref
  52.6 0.1 shard_map.101
  52.7 0.8 shard_map.102
  53.5 0.5 collective-permute-start.4
  53.9 1.2 %collective-permute-start.5 = (bf16[177,8,128]{2,1,0:T(8,128)(2,1)S(1)}, bf16[177,8,128]{2,1,0:T(8,128)(2,1)S(1)}, u32[]{:S(2)}, u32[]{:S(2)}) collective-permute-start(bf16[177,8,128]{2,1,0:T(8,128)(2,1)S(1)} %shard_map.96), channel_id=1, source_target_pairs={{0,2},{2,4},{4,6},{6,0},{1,3},{3,5},{5,7},{7,1},{8,10},{10,12},{12... | collective-permute-start | bytes 1087496 | tf_op jit(solution)/shard_map/ppermute | solution.py:497
  55.1 1.5 %collective-permute-start.7 = (bf16[128,1152]{1,0:T(8,128)(2,1)S(1)}, bf16[128,1152]{1,0:T(8,128)(2,1)S(1)}, u32[]{:S(2)}, u32[]{:S(2)}) collective-permute-start(bf16[128,1152]{1,0:T(8,128)(2,1)S(1)} %shard_map.97), channel_id=1, source_target_pairs={{0,6},{2,0},{4,2},{6,4},{1,7},{3,1},{5,3},{7,5},{8,14},{10,8},{12,... | collective-permute-start | bytes 884744 | tf_op jit(solution)/shard_map/ppermute | solution.py:497
  56.6 0.7 shard_map.103
  57.3 0.8 collective-permute-start.6
  58.0 0.0 collective-permute-start.11
  58.1 6.9 %collective-permute-done.5.refs_1_ = bf16[177,8,128]{2,1,0:T(8,128)(2,1)S(1)} collective-permute-done((bf16[177,8,128]{2,1,0:T(8,128)(2,1)S(1)}, bf16[177,8,128]{2,1,0:T(8,128)(2,1)S(1)}, u32[]{:S(2)}, u32[]{:S(2)}) %collective-permute-start.5) | collective-permute-done | bytes 362528 | tf_op jit(solution)/shard_map/ppermute | solution.py:497
  65.0 0.1 shard_map.104
  65.1 0.1 shard_map.105
  65.3 1.0 %shard_map.106 = (bf16[256,640]{1,0:T(8,128)(2,1)S(1)}, f32[8,128]{1,0:T(8,128)S(1)}) custom-call(s32[5]{0:T(128)S(1)} %stack.23.idx_ref, bf16[128,640]{1,0:T(8,128)(2,1)S(1)} %get-tuple-element.93.p_ref, f32[1,640]{1,0:T(1,128)S(1)} %reshape.gain_ref, bf16[1024,128]{1,0:T(8,128)(2,1)S(1)} %copy-done, bf16[256,640]{1,0:T(8,128)(2,1)S(1)} %copy-done.1, ...), custom_call_target="tpu_custom_call" | custom-call | flops 500000000 | tf_op jit(solution)/shard_map/pallas_call | solution.py:365
  66.2 0.8 shard_map.107
  67.0 1.7 %collective-permute-start.8 = (bf16[136,1408]{1,0:T(8,128)(2,1)S(1)}, bf16[136,1408]{1,0:T(8,128)(2,1)S(1)}, u32[]{:S(2)}, u32[]{:S(2)}) collective-permute-start(bf16[136,1408]{1,0:T(8,128)(2,1)S(1)} %get-tuple-element.99), channel_id=1, source_target_pairs={{0,1},{1,0},{2,3},{3,2},{4,5},{5,4},{6,7},{7,6},{8,9},{9,8},{10,11... | collective-permute-start | bytes 1148936 | tf_op jit(solution)/shard_map/ppermute | solution.py:518
  68.7 1.3 %collective-permute-start.10 = (bf16[177,8,128]{2,1,0:T(8,128)(2,1)S(1)}, bf16[177,8,128]{2,1,0:T(8,128)(2,1)S(1)}, u32[]{:S(2)}, u32[]{:S(2)}) collective-permute-start(bf16[177,8,128]{2,1,0:T(8,128)(2,1)S(1)} %shard_map.100), channel_id=1, source_target_pairs={{0,6},{2,0},{4,2},{6,4},{1,7},{3,1},{5,3},{7,5},{8,14},{10,8},{12,... | collective-permute-start | bytes 1087496 | tf_op jit(solution)/shard_map/ppermute | solution.py:504
  70.0 0.2 collective-permute-start.12
  70.2 0.7 shard_map.108
  70.9 0.7 collective-permute-start.9
  71.6 2.5 %collective-permute-start.13 = (bf16[128,1152]{1,0:T(8,128)(2,1)S(1)}, bf16[128,1152]{1,0:T(8,128)(2,1)S(1)}, u32[]{:S(2)}, u32[]{:S(2)}) collective-permute-start(bf16[128,1152]{1,0:T(8,128)(2,1)S(1)} %shard_map.105), channel_id=1, source_target_pairs={{0,6},{2,0},{4,2},{6,4},{1,7},{3,1},{5,3},{7,5},{8,14},{10,8},{12,... | collective-permute-start | bytes 884744 | tf_op jit(solution)/shard_map/ppermute | solution.py:514
  74.1 4.6 %collective-permute-done.10.la_ref = bf16[177,8,128]{2,1,0:T(8,128)(2,1)S(1)} collective-permute-done((bf16[177,8,128]{2,1,0:T(8,128)(2,1)S(1)}, bf16[177,8,128]{2,1,0:T(8,128)(2,1)S(1)}, u32[]{:S(2)}, u32[]{:S(2)}) %collective-permute-start.10) | collective-permute-done | bytes 362528 | tf_op jit(solution)/shard_map/ppermute | solution.py:504
  78.6 0.2 shard_map.109
  78.8 6.1 %collective-permute-done.13.lb_ref = bf16[128,1152]{1,0:T(8,128)(2,1)S(1)} collective-permute-done((bf16[128,1152]{1,0:T(8,128)(2,1)S(1)}, bf16[128,1152]{1,0:T(8,128)(2,1)S(1)}, u32[]{:S(2)}, u32[]{:S(2)}) %collective-permute-start.13) | collective-permute-done | bytes 294944 | tf_op jit(solution)/shard_map/ppermute | solution.py:514
  85.0 1.1 %shard_map.110 = bf16[128,2560]{1,0:T(8,128)(2,1)} custom-call(f32[8,128]{1,0:T(8,128)S(1)} %get-tuple-element.103.total_ref, f32[128,2560]{1,0:T(8,128)S(1)} %get-tuple-element.104.base_ref, bf16[177,8,128]{2,1,0:T(8,128)(2,1)S(1)} %collective-permute-done.12.ra_ref, bf16[128,1152]{1,0:T(8,128)(2,1)S(1)} %collective-permute-done.13.lb_ref), custom_call_target="tpu_custom_call" | custom-call | flops 100000000 | tf_op jit(solution)/shard_map/pallas_call | solution.py:365
  (18 shorter events, 0.0 us)
Async XLA Ops:
  0.0 29.9 %copy-start.3 = (bf16[640]{0:T(1024)(128)(2,1)S(1)}, bf16[640]{0:T(1024)(128)(2,1)}, u32[]{:S(2)}) copy-start(bf16[640]{0:T(1024)(128)(2,1)} %param.16) | copy-start | bytes 3844
  0.0 29.9 %copy-start.4 = (f32[10]{0:T(128)S(1)}, f32[10]{0:T(128)}, u32[]{:S(2)}) copy-start(f32[10]{0:T(128)} %param.15) | copy-start | bytes 124
  25.2 14.2 %all-to-all-start.1 = ((bf16[32,4,640]{2,1,0:T(4,128)(2,1)}), bf16[32,4,640]{2,1,0:T(4,128)(2,1)S(1)}, u32[]{:S(2)}, u32[]{:S(2)}) async-start(bf16[32,4,640]{2,1,0:T(4,128)(2,1)} %shard_map.92), calls=%async_computation.1 | async-start | bytes 327680 | tf_op jit(solution)/shard_map/all_to_all | solution.py:485
  30.2 9.3 %copy-start = (bf16[1024,128]{1,0:T(8,128)(2,1)S(1)}, bf16[1024,128]{1,0:T(8,128)(2,1)}, u32[]{:S(2)}) copy-start(bf16[1024,128]{1,0:T(8,128)(2,1)} %c_ref.7) | copy-start | bytes 786436
  41.3 6.4 %collective-permute-start = (bf16[136,1408]{1,0:T(8,128)(2,1)S(1)}, bf16[136,1408]{1,0:T(8,128)(2,1)S(1)}, u32[]{:S(2)}, u32[]{:S(2)}) collective-permute-start(bf16[136,1408]{1,0:T(8,128)(2,1)S(1)} %get-tuple-element.63), channel_id=1, source_target_pairs={{0,1},{1,0},{2,3},{3,2},{4,5},{5,4},{6,7},{7,6},{8,9},{9,8},{10,11... | collective-permute-start | bytes 1148936 | tf_op jit(solution)/shard_map/ppermute | solution.py:490
  47.6 1.7 %collective-permute-start.1 = (bf16[128,1152]{1,0:T(8,128)(2,1)S(1)}, bf16[128,1152]{1,0:T(8,128)(2,1)S(1)}, u32[]{:S(2)}, u32[]{:S(2)}) collective-permute-start(bf16[128,1152]{1,0:T(8,128)(2,1)S(1)} %get-tuple-element.71), channel_id=1, source_target_pairs={{0,1},{1,0},{2,3},{3,2},{4,5},{5,4},{6,7},{7,6},{8,9},{9,8},{10,11... | collective-permute-start | bytes 884744 | tf_op jit(solution)/shard_map/ppermute | solution.py:494
  50.1 1.8 %collective-permute-start.2 = (bf16[136,1408]{1,0:T(8,128)(2,1)S(1)}, bf16[136,1408]{1,0:T(8,128)(2,1)S(1)}, u32[]{:S(2)}, u32[]{:S(2)}) collective-permute-start(bf16[136,1408]{1,0:T(8,128)(2,1)S(1)} %get-tuple-element.76), channel_id=1, source_target_pairs={{0,1},{1,0},{2,3},{3,2},{4,5},{5,4},{6,7},{7,6},{8,9},{9,8},{10,11... | collective-permute-start | bytes 1148936 | tf_op jit(solution)/shard_map/ppermute | solution.py:500
  50.9 1.7 %collective-permute-start.3 = (bf16[128,1152]{1,0:T(8,128)(2,1)S(1)}, bf16[128,1152]{1,0:T(8,128)(2,1)S(1)}, u32[]{:S(2)}, u32[]{:S(2)}) collective-permute-start(bf16[128,1152]{1,0:T(8,128)(2,1)S(1)} %get-tuple-element.82), channel_id=1, source_target_pairs={{0,1},{1,0},{2,3},{3,2},{4,5},{5,4},{6,7},{7,6},{8,9},{9,8},{10,11... | collective-permute-start | bytes 884744 | tf_op jit(solution)/shard_map/ppermute | solution.py:502
  53.5 11.5 %collective-permute-start.4 = (bf16[136,1408]{1,0:T(8,128)(2,1)S(1)}, bf16[136,1408]{1,0:T(8,128)(2,1)S(1)}, u32[]{:S(2)}, u32[]{:S(2)}) collective-permute-start(bf16[136,1408]{1,0:T(8,128)(2,1)S(1)} %get-tuple-element.86), channel_id=1, source_target_pairs={{0,1},{1,0},{2,3},{3,2},{4,5},{5,4},{6,7},{7,6},{8,9},{9,8},{10,11... | collective-permute-start | bytes 1148936 | tf_op jit(solution)/shard_map/ppermute | solution.py:508
  53.9 11.1 %collective-permute-start.5 = (bf16[177,8,128]{2,1,0:T(8,128)(2,1)S(1)}, bf16[177,8,128]{2,1,0:T(8,128)(2,1)S(1)}, u32[]{:S(2)}, u32[]{:S(2)}) collective-permute-start(bf16[177,8,128]{2,1,0:T(8,128)(2,1)S(1)} %shard_map.96), channel_id=1, source_target_pairs={{0,2},{2,4},{4,6},{6,0},{1,3},{3,5},{5,7},{7,1},{8,10},{10,12},{12... | collective-permute-start | bytes 1087496 | tf_op jit(solution)/shard_map/ppermute | solution.py:497
  55.1 10.0 %collective-permute-start.7 = (bf16[128,1152]{1,0:T(8,128)(2,1)S(1)}, bf16[128,1152]{1,0:T(8,128)(2,1)S(1)}, u32[]{:S(2)}, u32[]{:S(2)}) collective-permute-start(bf16[128,1152]{1,0:T(8,128)(2,1)S(1)} %shard_map.97), channel_id=1, source_target_pairs={{0,6},{2,0},{4,2},{6,4},{1,7},{3,1},{5,3},{7,5},{8,14},{10,8},{12,... | collective-permute-start | bytes 884744 | tf_op jit(solution)/shard_map/ppermute | solution.py:497
  57.3 7.9 %collective-permute-start.6 = (bf16[128,1152]{1,0:T(8,128)(2,1)S(1)}, bf16[128,1152]{1,0:T(8,128)(2,1)S(1)}, u32[]{:S(2)}, u32[]{:S(2)}) collective-permute-start(bf16[128,1152]{1,0:T(8,128)(2,1)S(1)} %get-tuple-element.90), channel_id=1, source_target_pairs={{0,1},{1,0},{2,3},{3,2},{4,5},{5,4},{6,7},{7,6},{8,9},{9,8},{10,11... | collective-permute-start | bytes 884744 | tf_op jit(solution)/shard_map/ppermute | solution.py:510
  58.0 13.6 %collective-permute-start.11 = (bf16[128,1152]{1,0:T(8,128)(2,1)S(1)}, bf16[128,1152]{1,0:T(8,128)(2,1)S(1)}, u32[]{:S(2)}, u32[]{:S(2)}) collective-permute-start(bf16[128,1152]{1,0:T(8,128)(2,1)S(1)} %shard_map.101), channel_id=1, source_target_pairs={{0,2},{2,4},{4,6},{6,0},{1,3},{3,5},{5,7},{7,1},{8,10},{10,12},{12... | collective-permute-start | bytes 884744 | tf_op jit(solution)/shard_map/ppermute | solution.py:506
  58.0 7.2 %copy-start.1 = (bf16[256,640]{1,0:T(8,128)(2,1)S(1)}, bf16[256,640]{1,0:T(8,128)(2,1)}, u32[]{:S(2)}) copy-start(bf16[256,640]{1,0:T(8,128)(2,1)} %get-tuple-element.94.gl_ref) | copy-start | bytes 983044
  58.1 7.2 %copy-start.2 = (bf16[256,640]{1,0:T(8,128)(2,1)S(1)}, bf16[256,640]{1,0:T(8,128)(2,1)}, u32[]{:S(2)}) copy-start(bf16[256,640]{1,0:T(8,128)(2,1)} %get-tuple-element.95.fs_ref) | copy-start | bytes 983044
  67.0 11.6 %collective-permute-start.8 = (bf16[136,1408]{1,0:T(8,128)(2,1)S(1)}, bf16[136,1408]{1,0:T(8,128)(2,1)S(1)}, u32[]{:S(2)}, u32[]{:S(2)}) collective-permute-start(bf16[136,1408]{1,0:T(8,128)(2,1)S(1)} %get-tuple-element.99), channel_id=1, source_target_pairs={{0,1},{1,0},{2,3},{3,2},{4,5},{5,4},{6,7},{7,6},{8,9},{9,8},{10,11... | collective-permute-start | bytes 1148936 | tf_op jit(solution)/shard_map/ppermute | solution.py:518
  68.7 9.9 %collective-permute-start.10 = (bf16[177,8,128]{2,1,0:T(8,128)(2,1)S(1)}, bf16[177,8,128]{2,1,0:T(8,128)(2,1)S(1)}, u32[]{:S(2)}, u32[]{:S(2)}) collective-permute-start(bf16[177,8,128]{2,1,0:T(8,128)(2,1)S(1)} %shard_map.100), channel_id=1, source_target_pairs={{0,6},{2,0},{4,2},{6,4},{1,7},{3,1},{5,3},{7,5},{8,14},{10,8},{12,... | collective-permute-start | bytes 1087496 | tf_op jit(solution)/shard_map/ppermute | solution.py:504
  70.0 15.0 %collective-permute-start.12 = (bf16[177,8,128]{2,1,0:T(8,128)(2,1)S(1)}, bf16[177,8,128]{2,1,0:T(8,128)(2,1)S(1)}, u32[]{:S(2)}, u32[]{:S(2)}) collective-permute-start(bf16[177,8,128]{2,1,0:T(8,128)(2,1)S(1)} %shard_map.104), channel_id=1, source_target_pairs={{0,2},{2,4},{4,6},{6,0},{1,3},{3,5},{5,7},{7,1},{8,10},{10,12},{12... | collective-permute-start | bytes 1087496 | tf_op jit(solution)/shard_map/ppermute | solution.py:512
  70.9 7.8 %collective-permute-start.9 = (bf16[128,1152]{1,0:T(8,128)(2,1)S(1)}, bf16[128,1152]{1,0:T(8,128)(2,1)S(1)}, u32[]{:S(2)}, u32[]{:S(2)}) collective-permute-start(bf16[128,1152]{1,0:T(8,128)(2,1)S(1)} %get-tuple-element.102), channel_id=1, source_target_pairs={{0,1},{1,0},{2,3},{3,2},{4,5},{5,4},{6,7},{7,6},{8,9},{9,8},{10,11... | collective-permute-start | bytes 884744 | tf_op jit(solution)/shard_map/ppermute | solution.py:520
  71.6 13.4 %collective-permute-start.13 = (bf16[128,1152]{1,0:T(8,128)(2,1)S(1)}, bf16[128,1152]{1,0:T(8,128)(2,1)S(1)}, u32[]{:S(2)}, u32[]{:S(2)}) collective-permute-start(bf16[128,1152]{1,0:T(8,128)(2,1)S(1)} %shard_map.105), channel_id=1, source_target_pairs={{0,6},{2,0},{4,2},{6,4},{1,7},{3,1},{5,3},{7,5},{8,14},{10,8},{12,... | collective-permute-start | bytes 884744 | tf_op jit(solution)/shard_map/ppermute | solution.py:514
